TPU v7x, 1024 devices: a whole 4x4x32 slice. The times are simulated.
1024 devices in a mesh: dp: 128 (over y, z), mp: 8 (over x, core).
Axes of the slice: x: 4, y: 4, z: 32, core: 2. Of those that a mesh axis runs over, the one named last changes fastest.
Arguments:
- tokens_in: bfloat16 [131072, 512], P('dp'), may hold values from -24 to 24
- out_grad: bfloat16 [131072, 8192], P('dp', 'mp'), may hold values from -0.015625 to 0.015625
- left_root: bfloat16 [512, 8192], P(None, 'mp'), may hold values from -1 to 31
- right_root: bfloat16 [512, 8192], P(None, 'mp'), may hold values from -1 to 31
- master: float32 [512, 8192], P('dp', 'mp'), may hold values from -3 to 3
Outputs:
- new_weight: float32 [512, 8192], P('dp', 'mp')
All inputs are finite; a program needn't handle non-finite values.
Results may differ from a plain program's by a relative error of at most 0.0003.
Values sent between devices are 32-bit elements; how exact they have to be, the bound alone decides.
No kernel may reach another device: no remote copies, remote signals or barrier semaphores. Data moves between devices by JAX's collectives and lax.ppermute only.
A program may use at most 32 MiB of HBM per device.

v0:
```python
import jax
import jax.numpy as jnp
from jax import lax
from jax.sharding import Mesh
from jax.sharding import PartitionSpec as P

BLOCK = 512
DP = ("dp_0", "dp_1")
DP_MP = ("dp_0", "dp_1", "mp_0", "mp_1")
MP = ("mp_0", "mp_1")


clip_rms = 10.0
step_size = 0.25
epsilon = 1e-06


def sum_by_axis(running, axes):
    for axis in axes:
        running = lax.psum_scatter(running, axis, scatter_dimension=0, tiled=True)
    return running


def by_axis(array, axes):
    for axis in axes:
        array = lax.psum(array, axis)
    return array


def on_device(tokens_in, out_grad, left_root, right_root, master):
    rows_dev = master.shape[0]
    cols_dev = master.shape[1]
    win_rows = tokens_in.shape[1]
    col_blocks = cols_dev // BLOCK
    row_blocks = win_rows // BLOCK
    right_block = right_root
    right_block = right_block.astype(jnp.float32).reshape(BLOCK, col_blocks, BLOCK)
    partial_grad = lax.dot_general(
        tokens_in, out_grad, (((0,), (0,)), ((), ())), preferred_element_type=jnp.float32
    )
    left_full = left_root.astype(jnp.float32).reshape(row_blocks, BLOCK, col_blocks, BLOCK)
    premixed = jnp.einsum(
        "irck,ikcj->ircj",
        left_full,
        partial_grad.reshape(row_blocks, BLOCK, col_blocks, BLOCK),
        precision=lax.Precision.HIGHEST,
    )
    premixed = premixed.reshape(win_rows, cols_dev)
    own_rows = sum_by_axis(premixed, DP)
    right_mixed = jnp.einsum(
        "rck,kcj->rcj",
        own_rows.reshape(rows_dev, col_blocks, BLOCK),
        right_block,
        precision=lax.Precision.HIGHEST,
    )
    right_mixed = right_mixed.reshape(rows_dev, cols_dev)
    squares = by_axis(jnp.sum(right_mixed * right_mixed), DP_MP)
    entries = jnp.float32(win_rows * cols_dev * lax.axis_size(MP))
    root_mean = jnp.sqrt(squares / entries + epsilon)
    factor = jnp.minimum(jnp.float32(1.0), clip_rms / root_mean)
    return master - step_size * factor * right_mixed


def solution(mesh):
    split = Mesh(mesh.devices.reshape(4, 32, 4, 2), ("dp_0", "dp_1", "mp_0", "mp_1"))
    in_specs = (P(DP, None), P(DP, MP), P(None, MP), P(None, MP), P(DP, MP))
    out_specs = P(DP, MP)
    return jax.shard_map(
        on_device, mesh=split, in_specs=in_specs, out_specs=out_specs, check_vma=False
    )
```

profile of v0, /device:TPU:1, one launch (start us, length us, event | category | flops | bytes accessed | tf_op | source)
XLA Modules:
  0.0 431.9 jit_solution(9758058144582700810)
XLA Ops:
  6.5 0.0 copy-start
  6.5 0.0 copy-start.1
  6.5 0.0 reduce-scatter.2.cloned.1.call-start
  6.5 1.6 copy-done
  8.1 2.5 fusion.6
  10.6 0.0 copy-done.1
  10.7 3.1 fusion.3
  13.8 2.9 copy.16
  16.7 0.0 copy-start.2
  16.7 0.0 copy-start.3
  16.7 0.0 reduce-scatter.2.cloned.1.call-update
  16.8 0.0 all-reduce.3.cloned.1.call-start
  16.8 55.9 %reduce-scatter.2.cloned.1.call-done = f32[128,1024]{1,0:T(8,128)} async-done(((f32[512,1024]{1,0:T(8,128)}), f32[128,1024]{1,0:T(8,128)}) %reduce-scatter.2.cloned.1.call-update) | async-done | bytes 524304 | tf_op jit(solution)/shard_map/reduce_scatter | solution.py:20
  72.7 0.0 all-reduce.3.cloned.1.call-update
  72.7 1.3 dynamic-slice
  74.7 246.6 %all-reduce.3.cloned.1.call-done = f32[128,1024]{1,0:T(8,128)} async-done(((f32[128,1024]{1,0:T(8,128)}), f32[128,1024]{1,0:T(8,128)}) %all-reduce.3.cloned.1.call-update) | async-done | bytes 524304
  321.3 0.8 constant_dynamic-slice_fusion
  322.0 0.0 copy-done.2
  322.0 1.1 multiply_reduce_fusion
  323.1 9.6 %psum.28 = f32[]{:T(128)} all-reduce(f32[]{:T(128)} %get-tuple-element.5), channel_id=1, replica_groups=mesh['dp_0'=4,'dp_1'=32,'mp_0'=4,'mp_1'=2] {'dp_0'}, use_global_device_ids=true, to_apply=%region_3.0 | all-reduce | flops 1 | bytes 8 | tf_op jit(solution)/shard_map/psum | solution.py:26
  332.7 40.9 %psum.29 = f32[]{:T(128)} all-reduce(f32[]{:T(128)} %psum.28), channel_id=1, replica_groups=mesh['dp_0'=4,'dp_1'=32,'mp_0'=4,'mp_1'=2] {'dp_1'}, use_global_device_ids=true, to_apply=%region_4.0 | all-reduce | flops 1 | bytes 8 | tf_op jit(solution)/shard_map/psum | solution.py:26
  373.6 9.0 %psum.30 = f32[]{:T(128)} all-reduce(f32[]{:T(128)} %psum.29), channel_id=1, replica_groups=mesh['dp_0'=4,'dp_1'=32,'mp_0'=4,'mp_1'=2] {'mp_0'}, use_global_device_ids=true, to_apply=%region_5.0 | all-reduce | flops 1 | bytes 8 | tf_op jit(solution)/shard_map/psum | solution.py:26
  382.6 41.2 %psum.31 = f32[]{:T(128)} all-reduce(f32[]{:T(128)} %psum.30), channel_id=1, replica_groups=mesh['dp_0'=4,'dp_1'=32,'mp_0'=4,'mp_1'=2] {'mp_1'}, use_global_device_ids=true, to_apply=%region_6.0 | all-reduce | flops 1 | bytes 8 | tf_op jit(solution)/shard_map/psum | solution.py:26
  424.5 0.0 copy-done.3
  424.5 0.6 sub.3
  (1 shorter events, 0.0 us)
Async XLA Ops:
  6.5 1.6 copy-start
  6.5 4.1 copy-start.1
  6.5 66.2 %reduce-scatter.2.cloned.1.call-start = ((), (), s32[]{:S(2)}) async-start(), calls=%async_computation.1 | async-start | bytes 2621440 | tf_op jit(solution)/shard_map/reduce_scatter | solution.py:20
  16.7 305.3 %copy-start.2 = (bf16[512,1024]{1,0:T(8,128)(2,1)S(1)}, bf16[512,1024]{1,0:T(8,128)(2,1)}, u32[]{:S(2)}) copy-start(bf16[512,1024]{1,0:T(8,128)(2,1)} %param.8) | copy-start | bytes 3145732
  16.7 407.7 %copy-start.3 = (f32[4,1024]{1,0:T(4,128)S(1)}, f32[4,1024]{1,0:T(4,128)}, u32[]{:S(2)}) copy-start(f32[4,1024]{1,0:T(4,128)} %param.9) | copy-start | bytes 49156
  16.8 304.5 %all-reduce.3.cloned.1.call-start = ((), (), s32[]{:S(2)}) async-start(), calls=%async_computation.2 | async-start | bytes 1048576
Sparse Core Ops, SparseCore 0:
  16.9 55.7 reduce-scatter.1
  75.0 246.1 all-reduce.2
where the time goes:
time: 432 us
  waiting for transfers between devices  303 us (70%)
  blocking collectives  101 us (23%)
  between operations  14.8 us (3%)
  matrix products  6.78 us (2%)
  local copies, waits for them, and re-layouts  6.58 us (2%)
    unnamed x3, waiting for transfers between devices  247 us
    psum x4, blocking collectives, by_axis(): array = lax.psum(array, axis)  101 us
    reduce_scatter x1, waiting for transfers between devices, sum_by_axis(): running = lax.psum_scatter(running, axis, scatter_dimension=0, tiled=True)  55.9 us
  transfers between devices with their start and end apart: 2, of which 2 were waited for; matrix products, arithmetic and copies ran while one was open for 0% of the time, Pallas kernels for 0%

commit v1 on v0

v1 whole, which is shorter than its diff:
```python
import jax
import jax.numpy as jnp
from jax import lax
from jax.experimental import pallas as pl
from jax.experimental.pallas import tpu as pltpu
from jax.sharding import Mesh
from jax.sharding import PartitionSpec as P

BLOCK = 512
Y, ZH, ZL, X, C = "dp_y", "dp_zh", "dp_zl", "mp_x", "mp_c"
DP = (Y, ZH, ZL)
MP = (X, C)
NY, NZH, NZL, NX, NC = 4, 16, 2, 4, 2
ROWS, COLS_DEV = 512, 1024
PEERS = NY * NX * NC
NZ = NZH * NZL
ENTRIES = 512 * 8192

clip_rms = 10.0
step_size = 0.25
epsilon = 1e-06

VMEM = pltpu.VMEM


def split(x):
    hi = x.astype(jnp.bfloat16)
    lo = (x - hi.astype(jnp.float32)).astype(jnp.bfloat16)
    return hi, lo


def dot(a, b):
    return jnp.dot(a, b, preferred_element_type=jnp.float32)


def grad_kernel(a_ref, b_ref, l_ref, o_ref):
    g = lax.dot_general(
        a_ref[...], b_ref[...], (((0,), (0,)), ((), ())), preferred_element_type=jnp.float32
    )
    hi, lo = split(g)
    left = l_ref[...]
    p = dot(left, hi) + dot(left, lo)
    o_ref[...] = p.reshape(NY, 1, ROWS // NY, BLOCK)


def mix_kernel(s_ref, r_ref, keep_ref, send_ref, ss_ref):
    zl = lax.axis_index(ZL)
    rows = jnp.sum(s_ref[...], axis=0)
    right = r_ref[:, pl.ds(pl.multiple_of(zl * BLOCK, BLOCK), BLOCK)]
    hi, lo = split(rows)
    p = dot(hi, right) + dot(lo, right)
    first, second = p[:4], p[4:]
    keep_ref[...] = jnp.where(zl == 0, first, second)
    send_ref[...] = jnp.where(zl == 0, second, first)
    sq = jnp.sum(p * p, axis=0, keepdims=True)
    part = sq[:, :128] + sq[:, 128:256] + sq[:, 256:384] + sq[:, 384:]
    ss_ref[...] = jnp.broadcast_to(part[None], ss_ref.shape)


def relay_kernel(s_ref, o_ref):
    o_ref[...] = jnp.broadcast_to(jnp.sum(s_ref[...], axis=0, keepdims=True), o_ref.shape)


def update_kernel(s_ref, m_ref, keep_ref, recv_ref, o_ref):
    zl = lax.axis_index(ZL)
    squares = jnp.sum(jnp.sum(s_ref[...], axis=0), axis=1, keepdims=True)
    root_mean = jnp.sqrt(squares / jnp.float32(ENTRIES) + epsilon)
    factor = jnp.minimum(jnp.float32(1.0), clip_rms / root_mean)
    scale = step_size * factor
    keep, recv = keep_ref[...], recv_ref[...]
    left = jnp.where(zl == 0, keep, recv)
    right = jnp.where(zl == 0, recv, keep)
    o_ref[:, :BLOCK] = m_ref[:, :BLOCK] - scale * left
    o_ref[:, BLOCK:] = m_ref[:, BLOCK:] - scale * right


def params(mib):
    return pltpu.CompilerParams(vmem_limit_bytes=mib * 1024 * 1024)


def whole(n):
    return [pl.BlockSpec(memory_space=VMEM)] * n


def f32(*shape):
    return jax.ShapeDtypeStruct(shape, jnp.float32)


def on_device(tokens_in, out_grad, left_root, right_root, master):
    partial = pl.pallas_call(
        grad_kernel,
        grid=(2,),
        in_specs=[
            pl.BlockSpec((1024, 512), lambda c: (0, 0)),
            pl.BlockSpec((1024, BLOCK), lambda c: (0, c)),
            pl.BlockSpec((BLOCK, BLOCK), lambda c: (0, c)),
        ],
        out_specs=pl.BlockSpec((NY, 1, ROWS // NY, BLOCK), lambda c: (0, c, 0, 0)),
        out_shape=f32(NY, NZL, ROWS // NY, BLOCK),
        compiler_params=params(24),
        name="grad",
    )(tokens_in, out_grad, left_root)
    terms = lax.all_to_all(
        partial.reshape(NY * NZL, ROWS // NY, BLOCK), (Y, ZL), 0, 0, tiled=True
    )
    rows = jnp.sum(terms, axis=0)
    terms = lax.all_to_all(rows.reshape(NZH, 8, BLOCK), ZH, 0, 0, tiled=True)
    keep, send, squares = pl.pallas_call(
        mix_kernel,
        in_specs=whole(2),
        out_specs=tuple(whole(3)),
        out_shape=(f32(4, BLOCK), f32(4, BLOCK), f32(PEERS, 1, 128)),
        compiler_params=params(8),
        name="mix",
    )(terms, right_root)
    recv = lax.ppermute(send, ZL, [(0, 1), (1, 0)])
    squares = lax.all_to_all(squares, (Y, X, C), 0, 0, tiled=True)
    squares = pl.pallas_call(
        relay_kernel,
        in_specs=whole(1),
        out_specs=pl.BlockSpec(memory_space=VMEM),
        out_shape=f32(NZ, 1, 128),
        compiler_params=params(4),
        name="relay",
    )(squares)
    squares = lax.all_to_all(squares, (ZH, ZL), 0, 0, tiled=True)
    return pl.pallas_call(
        update_kernel,
        in_specs=whole(4),
        out_specs=pl.BlockSpec(memory_space=VMEM),
        out_shape=f32(4, COLS_DEV),
        compiler_params=params(4),
        name="update",
    )(squares, master, keep, recv)


def solution(mesh):
    split_mesh = Mesh(mesh.devices.reshape(NY, NZH, NZL, NX, NC), (Y, ZH, ZL, X, C))
    in_specs = (P(DP, None), P(DP, MP), P(None, MP), P(None, MP), P(DP, MP))
    return jax.shard_map(
        on_device, mesh=split_mesh, in_specs=in_specs, out_specs=P(DP, MP), check_vma=False
    )
```

time: 432 us -> 148 us (0.34)
  waiting for transfers between devices: 303 us -> 18.2 us
  between operations: 14.8 us -> 0.04 us
  starting transfers between devices: 0.04 us -> 12.8 us
  blocking collectives: 101 us -> 108 us
  matrix products: 6.78 us -> 0 us
  Pallas kernels: 0 us -> 4.72 us
    unnamed x3 -> x0, waiting for transfers between devices: 247 us -> none
    all_to_all x0 -> x3, blocking collectives: none -> 108 us  [the longest x1 64.4 us: on_device(): terms = lax.all_to_all(rows.reshape(NZH, 8, BLOCK), ZH, 0, 0, tiled=True)]
    psum x4 -> x0, blocking collectives: 101 us -> none  [by_axis(): array = lax.psum(array, axis)]
    reduce_scatter x1 -> x0, waiting for transfers between devices: 55.9 us -> none  [sum_by_axis(): running = lax.psum_scatter(running, axis, scatter_dimension=0, tiled=True)]
    all_to_all x0 -> x1, waiting for transfers between devices: none -> 16.6 us  [on_device(): squares = lax.all_to_all(squares, (ZH, ZL), 0, 0, tiled=True)]
    all_to_all x0 -> x1, starting transfers between devices: none -> 9.62 us  [on_device(): squares = lax.all_to_all(squares, (ZH, ZL), 0, 0, tiled=True)]
    pallas_call x0 -> x4, Pallas kernels: none -> 4.72 us  [the longest x1 3.06 us: on_device(): pl.pallas_call(grad_kernel, grid=(2,), in_specs=[pl.BlockSpec((1024, 512)...]
where the time goes in v1:
time: 148 us
  blocking collectives  108 us (73%)
  waiting for transfers between devices  18.2 us (12%)
  starting transfers between devices  12.8 us (9%)
  Pallas kernels  4.72 us (3%)
  local copies, waits for them, and re-layouts  4.05 us (3%)
    all_to_all x1, blocking collectives, on_device(): terms = lax.all_to_all(rows.reshape(NZH, 8, BLOCK), ZH, 0, 0, tiled=True)  64.4 us
    all_to_all x1, blocking collectives, on_device(): lax.all_to_all(partial.reshape(NY * NZL, ROWS // NY, BLOCK), (Y, ZL), 0,...  22.6 us
    all_to_all x1, blocking collectives, on_device(): squares = lax.all_to_all(squares, (Y, X, C), 0, 0, tiled=True)  20.7 us
    all_to_all x1, waiting for transfers between devices, on_device(): squares = lax.all_to_all(squares, (ZH, ZL), 0, 0, tiled=True)  16.6 us
    all_to_all x1, starting transfers between devices, on_device(): squares = lax.all_to_all(squares, (ZH, ZL), 0, 0, tiled=True)  9.62 us
    unnamed x10, local copies, waits for them, and re-layouts  4.05 us
    ppermute x1, starting transfers between devices, on_device(): recv = lax.ppermute(send, ZL, [(0, 1), (1, 0)])  3.14 us
    pallas_call x1, Pallas kernels, on_device(): pl.pallas_call(grad_kernel, grid=(2,), in_specs=[pl.BlockSpec((1024, 512)...  3.06 us
  transfers between devices with their start and end apart: 2, of which 2 were waited for; matrix products, arithmetic and copies ran while one was open for 0% of the time, Pallas kernels for 0%

profile of v1, /device:TPU:1, one launch (start us, length us, event | category | flops | bytes accessed | tf_op | source)
XLA Modules:
  0.0 147.5 jit_solution(4540540391583788184)
XLA Ops:
  0.0 0.0 copy-start
  0.0 1.6 %copy-done = bf16[1024,1024]{1,0:T(8,128)(2,1)S(1)} copy-done((bf16[1024,1024]{1,0:T(8,128)(2,1)S(1)}, bf16[1024,1024]{1,0:T(8,128)(2,1)}, u32[]{:S(2)}) %copy-start) | copy-done | bytes 2097176
  1.6 0.0 copy-start.2
  1.6 1.2 copy-done.2
  2.8 0.0 copy-start.3
  2.8 1.2 copy-done.3
  4.0 3.1 %grad.1 = f32[4,2,128,512]{3,2,1,0:T(8,128)S(1)} custom-call(bf16[1024,512]{1,0:T(8,128)(2,1)S(1)} %copy-done.2, bf16[1024,1024]{1,0:T(8,128)(2,1)S(1)} %copy-done, bf16[512,1024]{1,0:T(8,128)(2,1)S(1)} %copy-done.3), custom_call_target="tpu_custom_call" | custom-call | tf_op jit(solution)/shard_map/grad/pallas_call | solution.py:90
  7.1 22.6 %all_to_all.20 = f32[8,128,512]{2,1,0:T(8,128)S(1)} all-to-all(f32[8,128,512]{2,1,0:T(8,128)S(1)} %bitcast.2), channel_id=1, replica_groups=mesh['dp_y'=4,'dp_zh'=16,'dp_zl'=2,'mp_x'=4,'mp_c'=2] {'dp_y','dp_zl'}, dimensions={0} | all-to-all | bytes 4194304 | tf_op jit(solution)/shard_map/all_to_all | solution.py:103
  29.7 0.0 copy-start.1
  29.7 0.0 copy-start.4
  29.7 0.2 reduce_sum.9
  29.9 64.4 %all_to_all.21.s_ref = f32[16,8,512]{2,1,0:T(8,128)S(1)} all-to-all(f32[16,8,512]{2,1,0:T(8,128)S(1)} %bitcast.3), channel_id=1, replica_groups=mesh['dp_y'=4,'dp_zh'=16,'dp_zl'=2,'mp_x'=4,'mp_c'=2] {'dp_zh'}, dimensions={0} | all-to-all | bytes 524288 | tf_op jit(solution)/shard_map/all_to_all | solution.py:107
  94.3 0.0 copy-done.1
  94.3 0.3 mix.1
  94.6 20.7 %all_to_all.22.s_ref = f32[32,1,128]{2,1,0:T(1,128)S(1)} all-to-all(f32[32,1,128]{2,1,0:T(1,128)S(1)} %get-tuple-element.8), channel_id=1, replica_groups=mesh['dp_y'=4,'dp_zh'=16,'dp_zl'=2,'mp_x'=4,'mp_c'=2] {'dp_y','mp_x','mp..., dimensions={0} | all-to-all | bytes 32768 | tf_op jit(solution)/shard_map/all_to_all | solution.py:117
  115.2 0.6 relay.1
  115.9 9.6 %all-to-all-start.3 = ((f32[32,1,128]{2,1,0:T(1,128)}), f32[32,1,128]{2,1,0:T(1,128)S(1)}, u32[]{:S(2)}, u32[]{:S(2)}) async-start(f32[32,1,128]{2,1,0:T(1,128)} %relay.1), calls=%async_computation.3 | async-start | bytes 32768 | tf_op jit(solution)/shard_map/all_to_all | solution.py:126
  125.5 3.1 %collective-permute-start = (f32[4,512]{1,0:T(4,128)S(1)}, f32[4,512]{1,0:T(4,128)S(1)}, u32[]{:S(2)}, u32[]{:S(2)}) collective-permute-start(f32[4,512]{1,0:T(4,128)S(1)} %get-tuple-element.10), channel_id=1, source_target_pairs={{0,8},{8,0},{1,9},{9,1},{2,10},{10,2},{3,11},{11,3},{4,12},{12,4},... | collective-permute-start | bytes 24584 | tf_op jit(solution)/shard_map/ppermute | solution.py:116
  128.6 1.5 %collective-permute-done.recv_ref = f32[4,512]{1,0:T(4,128)S(1)} collective-permute-done((f32[4,512]{1,0:T(4,128)S(1)}, f32[4,512]{1,0:T(4,128)S(1)}, u32[]{:S(2)}, u32[]{:S(2)}) %collective-permute-start) | collective-permute-done | bytes 8224 | tf_op jit(solution)/shard_map/ppermute | solution.py:116
  130.2 16.6 %all-to-all-done.3.s_ref = f32[32,1,128]{2,1,0:T(1,128)S(1)} async-done(((f32[32,1,128]{2,1,0:T(1,128)}), f32[32,1,128]{2,1,0:T(1,128)S(1)}, u32[]{:S(2)}, u32[]{:S(2)}) %all-to-all-start.3) | async-done | bytes 16416 | tf_op jit(solution)/shard_map/all_to_all | solution.py:126
  146.8 0.0 copy-done.4
  146.8 0.7 update.1
Async XLA Ops:
  0.0 1.6 %copy-start = (bf16[1024,1024]{1,0:T(8,128)(2,1)S(1)}, bf16[1024,1024]{1,0:T(8,128)(2,1)}, u32[]{:S(2)}) copy-start(bf16[1024,1024]{1,0:T(8,128)(2,1)} %b_ref.1) | copy-start | bytes 6291460
  1.6 1.2 copy-start.2
  2.8 1.2 copy-start.3
  29.7 64.6 %copy-start.1 = (bf16[512,1024]{1,0:T(8,128)(2,1)S(1)}, bf16[512,1024]{1,0:T(8,128)(2,1)}, u32[]{:S(2)}) copy-start(bf16[512,1024]{1,0:T(8,128)(2,1)} %r_ref.1) | copy-start | bytes 3145732
  29.7 117.1 %copy-start.4 = (f32[4,1024]{1,0:T(4,128)S(1)}, f32[4,1024]{1,0:T(4,128)}, u32[]{:S(2)}) copy-start(f32[4,1024]{1,0:T(4,128)} %m_ref.1) | copy-start | bytes 49156
  115.9 30.9 %all-to-all-start.3 = ((f32[32,1,128]{2,1,0:T(1,128)}), f32[32,1,128]{2,1,0:T(1,128)S(1)}, u32[]{:S(2)}, u32[]{:S(2)}) async-start(f32[32,1,128]{2,1,0:T(1,128)} %relay.1), calls=%async_computation.3 | async-start | bytes 32768 | tf_op jit(solution)/shard_map/all_to_all | solution.py:126
  125.5 4.7 %collective-permute-start = (f32[4,512]{1,0:T(4,128)S(1)}, f32[4,512]{1,0:T(4,128)S(1)}, u32[]{:S(2)}, u32[]{:S(2)}) collective-permute-start(f32[4,512]{1,0:T(4,128)S(1)} %get-tuple-element.10), channel_id=1, source_target_pairs={{0,8},{8,0},{1,9},{9,1},{2,10},{10,2},{3,11},{11,3},{4,12},{12,4},... | collective-permute-start | bytes 24584 | tf_op jit(solution)/shard_map/ppermute | solution.py:116

commit v2 on v1

--- a/solution.py
+++ b/solution.py
@@ -33,14 +33,26 @@
     return jnp.dot(a, b, preferred_element_type=jnp.float32)
 
 
-def grad_kernel(a_ref, b_ref, l_ref, o_ref):
-    g = lax.dot_general(
-        a_ref[...], b_ref[...], (((0,), (0,)), ((), ())), preferred_element_type=jnp.float32
-    )
-    hi, lo = split(g)
-    left = l_ref[...]
-    p = dot(left, hi) + dot(left, lo)
-    o_ref[...] = p.reshape(NY, 1, ROWS // NY, BLOCK)
+def grad_kernel(a_hbm, b_hbm, l_hbm, o_ref, a_ref, b_ref, l_ref, sem):
+    def columns(hbm, ref, c, k):
+        return pltpu.make_async_copy(hbm.at[:, pl.ds(c * BLOCK, BLOCK)], ref.at[c], sem.at[k])
+
+    tokens = pltpu.make_async_copy(a_hbm, a_ref, sem.at[0])
+    grads = [columns(b_hbm, b_ref, c, 1 + c) for c in range(2)]
+    lefts = [columns(l_hbm, l_ref, c, 3 + c) for c in range(2)]
+    for copy in (tokens, grads[0], lefts[0], grads[1], lefts[1]):
+        copy.start()
+    tokens.wait()
+    for c in range(2):
+        grads[c].wait()
+        g = lax.dot_general(
+            a_ref[...], b_ref[c], (((0,), (0,)), ((), ())), preferred_element_type=jnp.float32
+        )
+        hi, lo = split(g)
+        lefts[c].wait()
+        left = l_ref[c]
+        p = dot(left, hi) + dot(left, lo)
+        o_ref[:, c] = p.reshape(NY, ROWS // NY, BLOCK)
 
 
 def mix_kernel(s_ref, r_ref, keep_ref, send_ref, ss_ref):
@@ -89,15 +101,16 @@
 def on_device(tokens_in, out_grad, left_root, right_root, master):
     partial = pl.pallas_call(
         grad_kernel,
-        grid=(2,),
-        in_specs=[
-            pl.BlockSpec((1024, 512), lambda c: (0, 0)),
-            pl.BlockSpec((1024, BLOCK), lambda c: (0, c)),
-            pl.BlockSpec((BLOCK, BLOCK), lambda c: (0, c)),
+        in_specs=[pl.BlockSpec(memory_space=pltpu.HBM)] * 3,
+        out_specs=pl.BlockSpec(memory_space=VMEM),
+        out_shape=VMEM((NY, NZL, ROWS // NY, BLOCK), jnp.float32),
+        scratch_shapes=[
+            VMEM((1024, ROWS), jnp.bfloat16),
+            VMEM((2, 1024, BLOCK), jnp.bfloat16),
+            VMEM((2, BLOCK, BLOCK), jnp.bfloat16),
+            pltpu.SemaphoreType.DMA((5,)),
         ],
-        out_specs=pl.BlockSpec((NY, 1, ROWS // NY, BLOCK), lambda c: (0, c, 0, 0)),
-        out_shape=f32(NY, NZL, ROWS // NY, BLOCK),
-        compiler_params=params(24),
+        compiler_params=params(59),
         name="grad",
     )(tokens_in, out_grad, left_root)
     terms = lax.all_to_all(
@@ -119,7 +132,7 @@
         relay_kernel,
         in_specs=whole(1),
         out_specs=pl.BlockSpec(memory_space=VMEM),
-        out_shape=f32(NZ, 1, 128),
+        out_shape=VMEM((NZ, 1, 128), jnp.float32),
         compiler_params=params(4),
         name="relay",
     )(squares)

time: 148 us -> 145 us (0.980)
  local copies, waits for them, and re-layouts: 4.05 us -> 0.01 us
    unnamed x10 -> x4, local copies, waits for them, and re-layouts: 4.05 us -> 0.01 us
where the time goes in v2:
time: 145 us
  blocking collectives  108 us (74%)
  waiting for transfers between devices  18.2 us (13%)
  starting transfers between devices  12.7 us (9%)
  Pallas kernels  6.14 us (4%)
    all_to_all x1, blocking collectives, on_device(): terms = lax.all_to_all(rows.reshape(NZH, 8, BLOCK), ZH, 0, 0, tiled=True)  64.4 us
    all_to_all x1, blocking collectives, on_device(): lax.all_to_all(partial.reshape(NY * NZL, ROWS // NY, BLOCK), (Y, ZL), 0,...  22.6 us
    all_to_all x1, blocking collectives, on_device(): squares = lax.all_to_all(squares, (Y, X, C), 0, 0, tiled=True)  20.7 us
    all_to_all x1, waiting for transfers between devices, on_device(): squares = lax.all_to_all(squares, (ZH, ZL), 0, 0, tiled=True)  16.6 us
    all_to_all x1, starting transfers between devices, on_device(): squares = lax.all_to_all(squares, (ZH, ZL), 0, 0, tiled=True)  9.61 us
    pallas_call x1, Pallas kernels, on_device(): pl.pallas_call(grad_kernel, in_specs=[pl.BlockSpec(memory_space=pltpu.HBM...  4.48 us
    ppermute x1, starting transfers between devices, on_device(): recv = lax.ppermute(send, ZL, [(0, 1), (1, 0)])  3.14 us
  transfers between devices with their start and end apart: 2, of which 2 were waited for; matrix products, arithmetic and copies ran while one was open for 0% of the time, Pallas kernels for 0%

profile of v2, /device:TPU:1, one launch (start us, length us, event | category | flops | bytes accessed | tf_op | source)
XLA Modules:
  0.0 144.9 jit_solution(16727460654880613242)
XLA Ops:
  0.0 4.5 %grad.1 = f32[4,2,128,512]{3,2,1,0:T(8,128)S(1)} custom-call(bf16[1024,512]{1,0:T(8,128)(2,1)} %a_hbm.1, bf16[1024,1024]{1,0:T(8,128)(2,1)} %b_hbm.1, bf16[512,1024]{1,0:T(8,128)(2,1)} %l_hbm.1), custom_call_target="tpu_custom_call" | custom-call | tf_op jit(solution)/shard_map/grad/pallas_call | solution.py:102
  4.5 22.6 %all_to_all.20 = f32[8,128,512]{2,1,0:T(8,128)S(1)} all-to-all(f32[8,128,512]{2,1,0:T(8,128)S(1)} %bitcast.2), channel_id=1, replica_groups=mesh['dp_y'=4,'dp_zh'=16,'dp_zl'=2,'mp_x'=4,'mp_c'=2] {'dp_y','dp_zl'}, dimensions={0} | all-to-all | bytes 4194304 | tf_op jit(solution)/shard_map/all_to_all | solution.py:116
  27.1 0.0 copy-start
  27.1 0.0 copy-start.1
  27.1 0.2 reduce_sum.9
  27.3 64.4 %all_to_all.21.s_ref = f32[16,8,512]{2,1,0:T(8,128)S(1)} all-to-all(f32[16,8,512]{2,1,0:T(8,128)S(1)} %bitcast.3), channel_id=1, replica_groups=mesh['dp_y'=4,'dp_zh'=16,'dp_zl'=2,'mp_x'=4,'mp_c'=2] {'dp_zh'}, dimensions={0} | all-to-all | bytes 524288 | tf_op jit(solution)/shard_map/all_to_all | solution.py:120
  91.6 0.0 copy-done
  91.6 0.3 mix.1
  91.9 20.7 %all_to_all.22.s_ref = f32[32,1,128]{2,1,0:T(1,128)S(1)} all-to-all(f32[32,1,128]{2,1,0:T(1,128)S(1)} %get-tuple-element.8), channel_id=1, replica_groups=mesh['dp_y'=4,'dp_zh'=16,'dp_zl'=2,'mp_x'=4,'mp_c'=2] {'dp_y','mp_x','mp..., dimensions={0} | all-to-all | bytes 32768 | tf_op jit(solution)/shard_map/all_to_all | solution.py:130
  112.6 0.6 relay.1
  113.3 9.6 %all-to-all-start.3 = ((f32[32,1,128]{2,1,0:T(1,128)}), f32[32,1,128]{2,1,0:T(1,128)S(1)}, u32[]{:S(2)}, u32[]{:S(2)}) async-start(f32[32,1,128]{2,1,0:T(1,128)} %relay.1), calls=%async_computation.3 | async-start | bytes 32768 | tf_op jit(solution)/shard_map/all_to_all | solution.py:139
  122.9 3.1 %collective-permute-start = (f32[4,512]{1,0:T(4,128)S(1)}, f32[4,512]{1,0:T(4,128)S(1)}, u32[]{:S(2)}, u32[]{:S(2)}) collective-permute-start(f32[4,512]{1,0:T(4,128)S(1)} %get-tuple-element.10), channel_id=1, source_target_pairs={{0,8},{8,0},{1,9},{9,1},{2,10},{10,2},{3,11},{11,3},{4,12},{12,4},... | collective-permute-start | bytes 24584 | tf_op jit(solution)/shard_map/ppermute | solution.py:129
  126.0 1.5 %collective-permute-done.recv_ref = f32[4,512]{1,0:T(4,128)S(1)} collective-permute-done((f32[4,512]{1,0:T(4,128)S(1)}, f32[4,512]{1,0:T(4,128)S(1)}, u32[]{:S(2)}, u32[]{:S(2)}) %collective-permute-start) | collective-permute-done | bytes 8224 | tf_op jit(solution)/shard_map/ppermute | solution.py:129
  127.6 16.6 %all-to-all-done.3.s_ref = f32[32,1,128]{2,1,0:T(1,128)S(1)} async-done(((f32[32,1,128]{2,1,0:T(1,128)}), f32[32,1,128]{2,1,0:T(1,128)S(1)}, u32[]{:S(2)}, u32[]{:S(2)}) %all-to-all-start.3) | async-done | bytes 16416 | tf_op jit(solution)/shard_map/all_to_all | solution.py:139
  144.2 0.0 copy-done.1
  144.2 0.7 update.1
Async XLA Ops:
  27.1 64.6 %copy-start = (bf16[512,1024]{1,0:T(8,128)(2,1)S(1)}, bf16[512,1024]{1,0:T(8,128)(2,1)}, u32[]{:S(2)}) copy-start(bf16[512,1024]{1,0:T(8,128)(2,1)} %r_ref.1) | copy-start | bytes 3145732
  27.1 117.1 %copy-start.1 = (f32[4,1024]{1,0:T(4,128)S(1)}, f32[4,1024]{1,0:T(4,128)}, u32[]{:S(2)}) copy-start(f32[4,1024]{1,0:T(4,128)} %m_ref.1) | copy-start | bytes 49156
  113.3 30.9 %all-to-all-start.3 = ((f32[32,1,128]{2,1,0:T(1,128)}), f32[32,1,128]{2,1,0:T(1,128)S(1)}, u32[]{:S(2)}, u32[]{:S(2)}) async-start(f32[32,1,128]{2,1,0:T(1,128)} %relay.1), calls=%async_computation.3 | async-start | bytes 32768 | tf_op jit(solution)/shard_map/all_to_all | solution.py:139
  122.9 4.7 %collective-permute-start = (f32[4,512]{1,0:T(4,128)S(1)}, f32[4,512]{1,0:T(4,128)S(1)}, u32[]{:S(2)}, u32[]{:S(2)}) collective-permute-start(f32[4,512]{1,0:T(4,128)S(1)} %get-tuple-element.10), channel_id=1, source_target_pairs={{0,8},{8,0},{1,9},{9,1},{2,10},{10,2},{3,11},{11,3},{4,12},{12,4},... | collective-permute-start | bytes 24584 | tf_op jit(solution)/shard_map/ppermute | solution.py:129

commit v3 on v2

--- a/solution.py
+++ b/solution.py
@@ -7,13 +7,13 @@
 from jax.sharding import PartitionSpec as P
 
 BLOCK = 512
-Y, ZH, ZL, X, C = "dp_y", "dp_zh", "dp_zl", "mp_x", "mp_c"
-DP = (Y, ZH, ZL)
+Y, ZH, ZM, ZL, X, C = "dp_y", "dp_zh", "dp_zm", "dp_zl", "mp_x", "mp_c"
+DP = (Y, ZH, ZM, ZL)
 MP = (X, C)
-NY, NZH, NZL, NX, NC = 4, 16, 2, 4, 2
+NY, NZH, NZM, NZL, NX, NC = 4, 8, 2, 2, 4, 2
 ROWS, COLS_DEV = 512, 1024
 PEERS = NY * NX * NC
-NZ = NZH * NZL
+NZ = NZH * NZM * NZL
 ENTRIES = 512 * 8192
 
 clip_rms = 10.0
@@ -52,7 +52,9 @@
         lefts[c].wait()
         left = l_ref[c]
         p = dot(left, hi) + dot(left, lo)
-        o_ref[:, c] = p.reshape(NY, ROWS // NY, BLOCK)
+        p = p.reshape(NY, NZH, NZM, 8, BLOCK)
+        for m in range(NZM):
+            o_ref[:, c, m] = p[:, :, m]
 
 
 def mix_kernel(s_ref, r_ref, keep_ref, send_ref, ss_ref):
@@ -103,7 +105,7 @@
         grad_kernel,
         in_specs=[pl.BlockSpec(memory_space=pltpu.HBM)] * 3,
         out_specs=pl.BlockSpec(memory_space=VMEM),
-        out_shape=VMEM((NY, NZL, ROWS // NY, BLOCK), jnp.float32),
+        out_shape=VMEM((NY, NZL, NZM, NZH, 8, BLOCK), jnp.float32),
         scratch_shapes=[
             VMEM((1024, ROWS), jnp.bfloat16),
             VMEM((2, 1024, BLOCK), jnp.bfloat16),
@@ -116,6 +118,8 @@
     terms = lax.all_to_all(
         partial.reshape(NY * NZL, ROWS // NY, BLOCK), (Y, ZL), 0, 0, tiled=True
     )
+    rows = jnp.sum(terms, axis=0)
+    terms = lax.all_to_all(rows.reshape(NZM, NZH * 8, BLOCK), ZM, 0, 0, tiled=True)
     rows = jnp.sum(terms, axis=0)
     terms = lax.all_to_all(rows.reshape(NZH, 8, BLOCK), ZH, 0, 0, tiled=True)
     keep, send, squares = pl.pallas_call(
@@ -136,7 +140,7 @@
         compiler_params=params(4),
         name="relay",
     )(squares)
-    squares = lax.all_to_all(squares, (ZH, ZL), 0, 0, tiled=True)
+    squares = lax.all_to_all(squares, (ZH, ZM, ZL), 0, 0, tiled=True)
     return pl.pallas_call(
         update_kernel,
         in_specs=whole(4),
@@ -148,7 +152,7 @@
 
 
 def solution(mesh):
-    split_mesh = Mesh(mesh.devices.reshape(NY, NZH, NZL, NX, NC), (Y, ZH, ZL, X, C))
+    split_mesh = Mesh(mesh.devices.reshape(NY, NZH, NZM, NZL, NX, NC), (Y, ZH, ZM, ZL, X, C))
     in_specs = (P(DP, None), P(DP, MP), P(None, MP), P(None, MP), P(DP, MP))
     return jax.shard_map(
         on_device, mesh=split_mesh, in_specs=in_specs, out_specs=P(DP, MP), check_vma=False

time: 145 us -> 142 us (0.979)
  starting transfers between devices: 12.7 us -> 7.4 us
  blocking collectives: 108 us -> 110 us
    all_to_all x0 -> x1, blocking collectives: none -> 22.4 us  [on_device(): lax.all_to_all(rows.reshape(NZM, NZH * 8, BLOCK), ZM, 0, 0, tiled=True)]
    all_to_all x1, blocking collectives: 64.4 us -> 49.5 us  [on_device(): terms = lax.all_to_all(rows.reshape(NZH, 8, BLOCK), ZH, 0, 0, tiled=True)]
    all_to_all x1, starting transfers between devices: 9.61 us -> 4.26 us  [on_device(): squares = lax.all_to_all(squares, (ZH, ZM, ZL), 0, 0, tiled=True)]
    all_to_all x1, blocking collectives: 20.7 us -> 15.4 us  [on_device(): squares = lax.all_to_all(squares, (Y, X, C), 0, 0, tiled=True)]
where the time goes in v3:
time: 142 us
  blocking collectives  110 us (77%)
  waiting for transfers between devices  18.2 us (13%)
  starting transfers between devices  7.4 us (5%)
  Pallas kernels  6.14 us (4%)
    all_to_all x1, blocking collectives, on_device(): terms = lax.all_to_all(rows.reshape(NZH, 8, BLOCK), ZH, 0, 0, tiled=True)  49.5 us
    all_to_all x1, blocking collectives, on_device(): lax.all_to_all(partial.reshape(NY * NZL, ROWS // NY, BLOCK), (Y, ZL), 0,...  22.6 us
    all_to_all x1, blocking collectives, on_device(): lax.all_to_all(rows.reshape(NZM, NZH * 8, BLOCK), ZM, 0, 0, tiled=True)  22.4 us
    all_to_all x1, waiting for transfers between devices, on_device(): squares = lax.all_to_all(squares, (ZH, ZM, ZL), 0, 0, tiled=True)  16.6 us
    all_to_all x1, blocking collectives, on_device(): squares = lax.all_to_all(squares, (Y, X, C), 0, 0, tiled=True)  15.4 us
    pallas_call x1, Pallas kernels, on_device(): pl.pallas_call(grad_kernel, in_specs=[pl.BlockSpec(memory_space=pltpu.HBM...  4.48 us
    all_to_all x1, starting transfers between devices, on_device(): squares = lax.all_to_all(squares, (ZH, ZM, ZL), 0, 0, tiled=True)  4.26 us
    ppermute x1, starting transfers between devices, on_device(): recv = lax.ppermute(send, ZL, [(0, 1), (1, 0)])  3.14 us
  transfers between devices with their start and end apart: 2, of which 2 were waited for; matrix products, arithmetic and copies ran while one was open for 0% of the time, Pallas kernels for 0%

profile of v3, /device:TPU:1, one launch (start us, length us, event | category | flops | bytes accessed | tf_op | source)
XLA Modules:
  0.0 141.9 jit_solution(766684004159049569)
XLA Ops:
  0.0 4.5 %grad.1 = f32[4,2,2,8,8,512]{5,4,3,2,1,0:T(8,128)S(1)} custom-call(bf16[1024,512]{1,0:T(8,128)(2,1)} %a_hbm.1, bf16[1024,1024]{1,0:T(8,128)(2,1)} %b_hbm.1, bf16[512,1024]{1,0:T(8,128)(2,1)} %l_hbm.1), custom_call_target="tpu_custom_call" | custom-call | tf_op jit(solution)/shard_map/grad/pallas_call | solution.py:104
  4.5 22.6 %all_to_all.25 = f32[8,128,512]{2,1,0:T(8,128)S(1)} all-to-all(f32[8,128,512]{2,1,0:T(8,128)S(1)} %bitcast.3), channel_id=1, replica_groups=mesh['dp_y'=4,'dp_zh'=8,'dp_zm'=2,'dp_zl'=2,'mp_x'=4,'mp_c'=2] {'dp_y','..., dimensions={0} | all-to-all | bytes 4194304 | tf_op jit(solution)/shard_map/all_to_all | solution.py:118
  27.1 0.0 copy-start
  27.1 0.0 copy-start.1
  27.1 0.2 reduce_sum.18
  27.3 22.4 %all_to_all.26 = f32[2,64,512]{2,1,0:T(8,128)S(1)} all-to-all(f32[2,64,512]{2,1,0:T(8,128)S(1)} %bitcast.4), channel_id=1, replica_groups=mesh['dp_y'=4,'dp_zh'=8,'dp_zm'=2,'dp_zl'=2,'mp_x'=4,'mp_c'=2] {'dp_zm'}, dimensions={0} | all-to-all | bytes 524288 | tf_op jit(solution)/shard_map/all_to_all | solution.py:122
  49.7 49.5 %all_to_all.27.s_ref = f32[8,8,512]{2,1,0:T(8,128)S(1)} all-to-all(f32[8,8,512]{2,1,0:T(8,128)S(1)} %bitcast.5), channel_id=1, replica_groups=mesh['dp_y'=4,'dp_zh'=8,'dp_zm'=2,'dp_zl'=2,'mp_x'=4,'mp_c'=2] {'dp_zh'}, dimensions={0} | all-to-all | bytes 262144 | tf_op jit(solution)/shard_map/all_to_all | solution.py:124
  99.2 0.0 copy-done
  99.2 0.3 mix.1
  99.5 15.4 %all_to_all.28.s_ref = f32[32,1,128]{2,1,0:T(1,128)S(1)} all-to-all(f32[32,1,128]{2,1,0:T(1,128)S(1)} %get-tuple-element.8), channel_id=1, replica_groups=mesh['dp_y'=4,'dp_zh'=8,'dp_zm'=2,'dp_zl'=2,'mp_x'=4,'mp_c'=2] {'dp_y','..., dimensions={0} | all-to-all | bytes 32768 | tf_op jit(solution)/shard_map/all_to_all | solution.py:134
  114.9 0.6 relay.1
  115.6 4.3 %all-to-all-start.4 = ((f32[32,1,128]{2,1,0:T(1,128)}), f32[32,1,128]{2,1,0:T(1,128)S(1)}, u32[]{:S(2)}, u32[]{:S(2)}) async-start(f32[32,1,128]{2,1,0:T(1,128)} %relay.1), calls=%async_computation.4 | async-start | bytes 32768 | tf_op jit(solution)/shard_map/all_to_all | solution.py:143
  119.8 3.1 %collective-permute-start = (f32[4,512]{1,0:T(4,128)S(1)}, f32[4,512]{1,0:T(4,128)S(1)}, u32[]{:S(2)}, u32[]{:S(2)}) collective-permute-start(f32[4,512]{1,0:T(4,128)S(1)} %get-tuple-element.10), channel_id=1, source_target_pairs={{0,8},{8,0},{1,9},{9,1},{2,10},{10,2},{3,11},{11,3},{4,12},{12,4},... | collective-permute-start | bytes 24584 | tf_op jit(solution)/shard_map/ppermute | solution.py:133
  123.0 1.5 %collective-permute-done.recv_ref = f32[4,512]{1,0:T(4,128)S(1)} collective-permute-done((f32[4,512]{1,0:T(4,128)S(1)}, f32[4,512]{1,0:T(4,128)S(1)}, u32[]{:S(2)}, u32[]{:S(2)}) %collective-permute-start) | collective-permute-done | bytes 8224 | tf_op jit(solution)/shard_map/ppermute | solution.py:133
  124.5 16.6 %all-to-all-done.4.s_ref = f32[32,1,128]{2,1,0:T(1,128)S(1)} async-done(((f32[32,1,128]{2,1,0:T(1,128)}), f32[32,1,128]{2,1,0:T(1,128)S(1)}, u32[]{:S(2)}, u32[]{:S(2)}) %all-to-all-start.4) | async-done | bytes 16416 | tf_op jit(solution)/shard_map/all_to_all | solution.py:143
  141.1 0.0 copy-done.1
  141.1 0.7 update.1
  (1 shorter events, 0.0 us)
Async XLA Ops:
  27.1 72.2 %copy-start = (bf16[512,1024]{1,0:T(8,128)(2,1)S(1)}, bf16[512,1024]{1,0:T(8,128)(2,1)}, u32[]{:S(2)}) copy-start(bf16[512,1024]{1,0:T(8,128)(2,1)} %r_ref.1) | copy-start | bytes 3145732
  27.1 114.1 %copy-start.1 = (f32[4,1024]{1,0:T(4,128)S(1)}, f32[4,1024]{1,0:T(4,128)}, u32[]{:S(2)}) copy-start(f32[4,1024]{1,0:T(4,128)} %m_ref.1) | copy-start | bytes 49156
  115.6 25.6 %all-to-all-start.4 = ((f32[32,1,128]{2,1,0:T(1,128)}), f32[32,1,128]{2,1,0:T(1,128)S(1)}, u32[]{:S(2)}, u32[]{:S(2)}) async-start(f32[32,1,128]{2,1,0:T(1,128)} %relay.1), calls=%async_computation.4 | async-start | bytes 32768 | tf_op jit(solution)/shard_map/all_to_all | solution.py:143
  119.8 4.7 %collective-permute-start = (f32[4,512]{1,0:T(4,128)S(1)}, f32[4,512]{1,0:T(4,128)S(1)}, u32[]{:S(2)}, u32[]{:S(2)}) collective-permute-start(f32[4,512]{1,0:T(4,128)S(1)} %get-tuple-element.10), channel_id=1, source_target_pairs={{0,8},{8,0},{1,9},{9,1},{2,10},{10,2},{3,11},{11,3},{4,12},{12,4},... | collective-permute-start | bytes 24584 | tf_op jit(solution)/shard_map/ppermute | solution.py:133

commit v4 on v3

--- a/solution.py
+++ b/solution.py
@@ -13,6 +13,10 @@
 NY, NZH, NZM, NZL, NX, NC = 4, 8, 2, 2, 4, 2
 ROWS, COLS_DEV = 512, 1024
 PEERS = NY * NX * NC
+NEIGHBOURS = [
+    [y * 32 + z % 32 for y in range(4) for z in ((2 * k + 1, 2 * k + 2) if k % 2 == 0 else (2 * k + 2, 2 * k + 1))]
+    for k in range(16)
+]
 NZ = NZH * NZM * NZL
 ENTRIES = 512 * 8192
 
@@ -54,7 +58,7 @@
         p = dot(left, hi) + dot(left, lo)
         p = p.reshape(NY, NZH, NZM, 8, BLOCK)
         for m in range(NZM):
-            o_ref[:, c, m] = p[:, :, m]
+            o_ref[:, m, c] = p[:, :, m]
 
 
 def mix_kernel(s_ref, r_ref, keep_ref, send_ref, ss_ref):
@@ -105,7 +109,7 @@
         grad_kernel,
         in_specs=[pl.BlockSpec(memory_space=pltpu.HBM)] * 3,
         out_specs=pl.BlockSpec(memory_space=VMEM),
-        out_shape=VMEM((NY, NZL, NZM, NZH, 8, BLOCK), jnp.float32),
+        out_shape=VMEM((NY, NZM, NZL, NZH, 8, BLOCK), jnp.float32),
         scratch_shapes=[
             VMEM((1024, ROWS), jnp.bfloat16),
             VMEM((2, 1024, BLOCK), jnp.bfloat16),
@@ -116,31 +120,36 @@
         name="grad",
     )(tokens_in, out_grad, left_root)
     terms = lax.all_to_all(
-        partial.reshape(NY * NZL, ROWS // NY, BLOCK), (Y, ZL), 0, 0, tiled=True
+        partial.reshape(NY * NZM, ROWS // NY, BLOCK),
+        DP,
+        0,
+        0,
+        axis_index_groups=NEIGHBOURS,
+        tiled=True,
     )
     rows = jnp.sum(terms, axis=0)
-    terms = lax.all_to_all(rows.reshape(NZM, NZH * 8, BLOCK), ZM, 0, 0, tiled=True)
+    terms = lax.all_to_all(rows.reshape(NZL, NZH * 8, BLOCK), ZL, 0, 0, tiled=True)
     rows = jnp.sum(terms, axis=0)
     terms = lax.all_to_all(rows.reshape(NZH, 8, BLOCK), ZH, 0, 0, tiled=True)
     keep, send, squares = pl.pallas_call(
         mix_kernel,
         in_specs=whole(2),
         out_specs=tuple(whole(3)),
-        out_shape=(f32(4, BLOCK), f32(4, BLOCK), f32(PEERS, 1, 128)),
+        out_shape=(f32(4, BLOCK), f32(4, BLOCK), f32(NZ, 1, 128)),
         compiler_params=params(8),
         name="mix",
     )(terms, right_root)
     recv = lax.ppermute(send, ZL, [(0, 1), (1, 0)])
-    squares = lax.all_to_all(squares, (Y, X, C), 0, 0, tiled=True)
+    squares = lax.all_to_all(squares, (ZH, ZM, ZL), 0, 0, tiled=True)
     squares = pl.pallas_call(
         relay_kernel,
         in_specs=whole(1),
         out_specs=pl.BlockSpec(memory_space=VMEM),
-        out_shape=VMEM((NZ, 1, 128), jnp.float32),
+        out_shape=VMEM((PEERS, 1, 128), jnp.float32),
         compiler_params=params(4),
         name="relay",
     )(squares)
-    squares = lax.all_to_all(squares, (ZH, ZM, ZL), 0, 0, tiled=True)
+    squares = lax.all_to_all(squares, (Y, X, C), 0, 0, tiled=True)
     return pl.pallas_call(
         update_kernel,
         in_specs=whole(4),

time: 142 us -> 142 us (level)
  waiting for transfers between devices: 18.2 us -> 4.96 us
  blocking collectives: 110 us -> 120 us
  starting transfers between devices: 7.4 us -> 10.6 us
    all_to_all x3, blocking collectives: 60.4 us -> 85.8 us  [the longest x1 48.3 us: on_device(): lax.all_to_all(partial.reshape(NY * NZM, ROWS // NY, BLOCK), DP, 0, 0, ax...]
    all_to_all x1, blocking collectives: 49.5 us -> 33.9 us  [on_device(): terms = lax.all_to_all(rows.reshape(NZH, 8, BLOCK), ZH, 0, 0, tiled=True)]
    all_to_all x1, waiting for transfers between devices: 16.6 us -> 2.2 us  [on_device(): squares = lax.all_to_all(squares, (Y, X, C), 0, 0, tiled=True)]
    all_to_all x1, starting transfers between devices: 4.26 us -> 8.72 us  [on_device(): squares = lax.all_to_all(squares, (Y, X, C), 0, 0, tiled=True)]
where the time goes in v4:
time: 142 us
  blocking collectives  120 us (85%)
  starting transfers between devices  10.6 us (7%)
  Pallas kernels  6.14 us (4%)
  waiting for transfers between devices  4.96 us (3%)
    all_to_all x1, blocking collectives, on_device(): lax.all_to_all(partial.reshape(NY * NZM, ROWS // NY, BLOCK), DP, 0, 0, ax...  48.3 us
    all_to_all x1, blocking collectives, on_device(): terms = lax.all_to_all(rows.reshape(NZH, 8, BLOCK), ZH, 0, 0, tiled=True)  33.9 us
    all_to_all x1, blocking collectives, on_device(): squares = lax.all_to_all(squares, (ZH, ZM, ZL), 0, 0, tiled=True)  30.9 us
    all_to_all x1, starting transfers between devices, on_device(): squares = lax.all_to_all(squares, (Y, X, C), 0, 0, tiled=True)  8.72 us
    all_to_all x1, blocking collectives, on_device(): lax.all_to_all(rows.reshape(NZL, NZH * 8, BLOCK), ZL, 0, 0, tiled=True)  6.55 us
    pallas_call x1, Pallas kernels, on_device(): pl.pallas_call(grad_kernel, in_specs=[pl.BlockSpec(memory_space=pltpu.HBM...  4.48 us
  transfers between devices with their start and end apart: 2, of which 2 were waited for; matrix products, arithmetic and copies ran while one was open for 0% of the time, Pallas kernels for 0%

profile of v4, /device:TPU:1, one launch (start us, length us, event | category | flops | bytes accessed | tf_op | source)
XLA Modules:
  0.0 141.7 jit_solution(17776839671328011216)
XLA Ops:
  0.0 4.5 %grad.1 = f32[4,2,2,8,8,512]{5,4,3,2,1,0:T(8,128)S(1)} custom-call(bf16[1024,512]{1,0:T(8,128)(2,1)} %a_hbm.1, bf16[1024,1024]{1,0:T(8,128)(2,1)} %b_hbm.1, bf16[512,1024]{1,0:T(8,128)(2,1)} %l_hbm.1), custom_call_target="tpu_custom_call" | custom-call | tf_op jit(solution)/shard_map/grad/pallas_call | solution.py:108
  4.5 48.3 %all_to_all.25 = f32[8,128,512]{2,1,0:T(8,128)S(1)} all-to-all(f32[8,128,512]{2,1,0:T(8,128)S(1)} %bitcast.3), channel_id=1, replica_groups={{8,16,264,272,520,528,776,784},{32,24,288,280,544,536,800,792},{40,48,2..., dimensions={0} | all-to-all | bytes 4194304 | tf_op jit(solution)/shard_map/all_to_all | solution.py:122
  52.8 0.0 copy-start
  52.8 0.0 copy-start.1
  52.8 0.2 reduce_sum.18
  53.0 6.5 %all_to_all.26 = f32[2,64,512]{2,1,0:T(8,128)S(1)} all-to-all(f32[2,64,512]{2,1,0:T(8,128)S(1)} %bitcast.4), channel_id=1, replica_groups=mesh['dp_y'=4,'dp_zh'=8,'dp_zm'=2,'dp_zl'=2,'mp_x'=4,'mp_c'=2] {'dp_zl'}, dimensions={0} | all-to-all | bytes 524288 | tf_op jit(solution)/shard_map/all_to_all | solution.py:131
  59.6 33.9 %all_to_all.27.s_ref = f32[8,8,512]{2,1,0:T(8,128)S(1)} all-to-all(f32[8,8,512]{2,1,0:T(8,128)S(1)} %bitcast.5), channel_id=1, replica_groups=mesh['dp_y'=4,'dp_zh'=8,'dp_zm'=2,'dp_zl'=2,'mp_x'=4,'mp_c'=2] {'dp_zh'}, dimensions={0} | all-to-all | bytes 262144 | tf_op jit(solution)/shard_map/all_to_all | solution.py:133
  93.4 0.0 copy-done
  93.4 0.3 mix.1
  93.7 30.9 %all_to_all.28.s_ref = f32[32,1,128]{2,1,0:T(1,128)S(1)} all-to-all(f32[32,1,128]{2,1,0:T(1,128)S(1)} %get-tuple-element.8), channel_id=1, replica_groups=mesh['dp_y'=4,'dp_zh'=8,'dp_zm'=2,'dp_zl'=2,'mp_x'=4,'mp_c'=2] {'dp_zh',..., dimensions={0} | all-to-all | bytes 32768 | tf_op jit(solution)/shard_map/all_to_all | solution.py:143
  124.6 0.6 relay.1
  125.3 8.7 %all-to-all-start.4 = ((f32[32,1,128]{2,1,0:T(1,128)}), f32[32,1,128]{2,1,0:T(1,128)S(1)}, u32[]{:S(2)}, u32[]{:S(2)}) async-start(f32[32,1,128]{2,1,0:T(1,128)} %relay.1), calls=%async_computation.4 | async-start | bytes 32768 | tf_op jit(solution)/shard_map/all_to_all | solution.py:152
  134.0 1.9 %collective-permute-start = (f32[4,512]{1,0:T(4,128)S(1)}, f32[4,512]{1,0:T(4,128)S(1)}, u32[]{:S(2)}, u32[]{:S(2)}) collective-permute-start(f32[4,512]{1,0:T(4,128)S(1)} %get-tuple-element.10), channel_id=1, source_target_pairs={{0,8},{8,0},{1,9},{9,1},{2,10},{10,2},{3,11},{11,3},{4,12},{12,4},... | collective-permute-start | bytes 24584 | tf_op jit(solution)/shard_map/ppermute | solution.py:142
  136.0 2.8 %collective-permute-done.recv_ref = f32[4,512]{1,0:T(4,128)S(1)} collective-permute-done((f32[4,512]{1,0:T(4,128)S(1)}, f32[4,512]{1,0:T(4,128)S(1)}, u32[]{:S(2)}, u32[]{:S(2)}) %collective-permute-start) | collective-permute-done | bytes 8224 | tf_op jit(solution)/shard_map/ppermute | solution.py:142
  138.7 2.2 %all-to-all-done.4.s_ref = f32[32,1,128]{2,1,0:T(1,128)S(1)} async-done(((f32[32,1,128]{2,1,0:T(1,128)}), f32[32,1,128]{2,1,0:T(1,128)S(1)}, u32[]{:S(2)}, u32[]{:S(2)}) %all-to-all-start.4) | async-done | bytes 16416 | tf_op jit(solution)/shard_map/all_to_all | solution.py:152
  140.9 0.0 copy-done.1
  140.9 0.7 update.1
  (1 shorter events, 0.0 us)
Async XLA Ops:
  52.8 40.7 %copy-start = (bf16[512,1024]{1,0:T(8,128)(2,1)S(1)}, bf16[512,1024]{1,0:T(8,128)(2,1)}, u32[]{:S(2)}) copy-start(bf16[512,1024]{1,0:T(8,128)(2,1)} %r_ref.1) | copy-start | bytes 3145732
  52.8 88.1 %copy-start.1 = (f32[4,1024]{1,0:T(4,128)S(1)}, f32[4,1024]{1,0:T(4,128)}, u32[]{:S(2)}) copy-start(f32[4,1024]{1,0:T(4,128)} %m_ref.1) | copy-start | bytes 49156
  125.3 15.6 %all-to-all-start.4 = ((f32[32,1,128]{2,1,0:T(1,128)}), f32[32,1,128]{2,1,0:T(1,128)S(1)}, u32[]{:S(2)}, u32[]{:S(2)}) async-start(f32[32,1,128]{2,1,0:T(1,128)} %relay.1), calls=%async_computation.4 | async-start | bytes 32768 | tf_op jit(solution)/shard_map/all_to_all | solution.py:152
  134.0 4.7 %collective-permute-start = (f32[4,512]{1,0:T(4,128)S(1)}, f32[4,512]{1,0:T(4,128)S(1)}, u32[]{:S(2)}, u32[]{:S(2)}) collective-permute-start(f32[4,512]{1,0:T(4,128)S(1)} %get-tuple-element.10), channel_id=1, source_target_pairs={{0,8},{8,0},{1,9},{9,1},{2,10},{10,2},{3,11},{11,3},{4,12},{12,4},... | collective-permute-start | bytes 24584 | tf_op jit(solution)/shard_map/ppermute | solution.py:142

commit v5 on v4

--- a/solution.py
+++ b/solution.py
@@ -12,12 +12,11 @@
 MP = (X, C)
 NY, NZH, NZM, NZL, NX, NC = 4, 8, 2, 2, 4, 2
 ROWS, COLS_DEV = 512, 1024
-PEERS = NY * NX * NC
+PEERS = NY * NZM * NZL * NX * NC
 NEIGHBOURS = [
     [y * 32 + z % 32 for y in range(4) for z in ((2 * k + 1, 2 * k + 2) if k % 2 == 0 else (2 * k + 2, 2 * k + 1))]
     for k in range(16)
 ]
-NZ = NZH * NZM * NZL
 ENTRIES = 512 * 8192
 
 clip_rms = 10.0
@@ -58,38 +57,40 @@
         p = dot(left, hi) + dot(left, lo)
         p = p.reshape(NY, NZH, NZM, 8, BLOCK)
         for m in range(NZM):
-            o_ref[:, m, c] = p[:, :, m]
+            o_ref[:, m, :, :, pl.ds(c * BLOCK, BLOCK)] = p[:, :, m]
 
 
-def mix_kernel(s_ref, r_ref, keep_ref, send_ref, ss_ref):
-    zl = lax.axis_index(ZL)
+def fold_kernel(s_ref, o_ref):
     rows = jnp.sum(s_ref[...], axis=0)
-    right = r_ref[:, pl.ds(pl.multiple_of(zl * BLOCK, BLOCK), BLOCK)]
+    o_ref[0] = rows[:, :4]
+    o_ref[1] = rows[:, 4:]
+
+
+def mix_kernel(s_ref, r_ref, p_ref, ss_ref):
+    rows = jnp.sum(s_ref[...], axis=0)
     hi, lo = split(rows)
-    p = dot(hi, right) + dot(lo, right)
-    first, second = p[:4], p[4:]
-    keep_ref[...] = jnp.where(zl == 0, first, second)
-    send_ref[...] = jnp.where(zl == 0, second, first)
-    sq = jnp.sum(p * p, axis=0, keepdims=True)
-    part = sq[:, :128] + sq[:, 128:256] + sq[:, 256:384] + sq[:, 384:]
-    ss_ref[...] = jnp.broadcast_to(part[None], ss_ref.shape)
+    total = jnp.zeros((1, 128), jnp.float32)
+    for c in range(2):
+        cols = pl.ds(c * BLOCK, BLOCK)
+        right = r_ref[:, cols]
+        here = slice(c * BLOCK, (c + 1) * BLOCK)
+        p = dot(hi[:, here], right) + dot(lo[:, here], right)
+        p_ref[:, cols] = p
+        sq = jnp.sum(p * p, axis=0, keepdims=True)
+        total = total + (sq[:, :128] + sq[:, 128:256] + sq[:, 256:384] + sq[:, 384:])
+    ss_ref[...] = jnp.broadcast_to(total[None], ss_ref.shape)
 
 
 def relay_kernel(s_ref, o_ref):
-    o_ref[...] = jnp.broadcast_to(jnp.sum(s_ref[...], axis=0, keepdims=True), o_ref.shape)
+    o_ref[...] = jnp.sum(s_ref[...], axis=0)
 
 
-def update_kernel(s_ref, m_ref, keep_ref, recv_ref, o_ref):
-    zl = lax.axis_index(ZL)
+def update_kernel(s_ref, m_ref, p_ref, o_ref):
     squares = jnp.sum(jnp.sum(s_ref[...], axis=0), axis=1, keepdims=True)
     root_mean = jnp.sqrt(squares / jnp.float32(ENTRIES) + epsilon)
     factor = jnp.minimum(jnp.float32(1.0), clip_rms / root_mean)
     scale = step_size * factor
-    keep, recv = keep_ref[...], recv_ref[...]
-    left = jnp.where(zl == 0, keep, recv)
-    right = jnp.where(zl == 0, recv, keep)
-    o_ref[:, :BLOCK] = m_ref[:, :BLOCK] - scale * left
-    o_ref[:, BLOCK:] = m_ref[:, BLOCK:] - scale * right
+    o_ref[...] = m_ref[...] - scale * p_ref[...]
 
 
 def params(mib):
@@ -109,7 +110,7 @@
         grad_kernel,
         in_specs=[pl.BlockSpec(memory_space=pltpu.HBM)] * 3,
         out_specs=pl.BlockSpec(memory_space=VMEM),
-        out_shape=VMEM((NY, NZM, NZL, NZH, 8, BLOCK), jnp.float32),
+        out_shape=VMEM((NY, NZM, NZH, 8, COLS_DEV), jnp.float32),
         scratch_shapes=[
             VMEM((1024, ROWS), jnp.bfloat16),
             VMEM((2, 1024, BLOCK), jnp.bfloat16),
@@ -120,44 +121,50 @@
         name="grad",
     )(tokens_in, out_grad, left_root)
     terms = lax.all_to_all(
-        partial.reshape(NY * NZM, ROWS // NY, BLOCK),
+        partial.reshape(NY * NZM, NZH, 8, COLS_DEV),
         DP,
         0,
         0,
         axis_index_groups=NEIGHBOURS,
         tiled=True,
     )
+    rows = pl.pallas_call(
+        fold_kernel,
+        in_specs=whole(1),
+        out_specs=pl.BlockSpec(memory_space=VMEM),
+        out_shape=VMEM((NZL, NZH, 4, COLS_DEV), jnp.float32),
+        compiler_params=params(8),
+        name="fold",
+    )(terms)
+    terms = lax.all_to_all(rows, ZL, 0, 0, tiled=True)
     rows = jnp.sum(terms, axis=0)
-    terms = lax.all_to_all(rows.reshape(NZL, NZH * 8, BLOCK), ZL, 0, 0, tiled=True)
-    rows = jnp.sum(terms, axis=0)
-    terms = lax.all_to_all(rows.reshape(NZH, 8, BLOCK), ZH, 0, 0, tiled=True)
-    keep, send, squares = pl.pallas_call(
+    terms = lax.all_to_all(rows, ZH, 0, 0, tiled=True)
+    precond, squares = pl.pallas_call(
         mix_kernel,
         in_specs=whole(2),
-        out_specs=tuple(whole(3)),
-        out_shape=(f32(4, BLOCK), f32(4, BLOCK), f32(NZ, 1, 128)),
+        out_specs=tuple(whole(2)),
+        out_shape=(f32(4, COLS_DEV), VMEM((PEERS, 1, 128), jnp.float32)),
         compiler_params=params(8),
         name="mix",
     )(terms, right_root)
-    recv = lax.ppermute(send, ZL, [(0, 1), (1, 0)])
-    squares = lax.all_to_all(squares, (ZH, ZM, ZL), 0, 0, tiled=True)
+    squares = lax.all_to_all(squares, (Y, ZM, ZL, X, C), 0, 0, tiled=True)
     squares = pl.pallas_call(
         relay_kernel,
         in_specs=whole(1),
         out_specs=pl.BlockSpec(memory_space=VMEM),
-        out_shape=VMEM((PEERS, 1, 128), jnp.float32),
+        out_shape=VMEM((1, 128), jnp.float32),
         compiler_params=params(4),
         name="relay",
     )(squares)
-    squares = lax.all_to_all(squares, (Y, X, C), 0, 0, tiled=True)
+    squares = lax.all_gather(squares, ZH)
     return pl.pallas_call(
         update_kernel,
-        in_specs=whole(4),
+        in_specs=whole(3),
         out_specs=pl.BlockSpec(memory_space=VMEM),
         out_shape=f32(4, COLS_DEV),
         compiler_params=params(4),
         name="update",
-    )(squares, master, keep, recv)
+    )(squares, master, precond)
 
 
 def solution(mesh):

time: 142 us -> 139 us (0.979); the launches traced: 142 us -> 137 us
  blocking collectives: 120 us -> 131 us
  starting transfers between devices: 10.6 us -> 0 us
  waiting for transfers between devices: 4.96 us -> 0 us
    all_gather x0 -> x1, blocking collectives: none -> 15.9 us  [on_device(): squares = lax.all_gather(squares, ZH)]
    all_to_all x1 -> x0, starting transfers between devices: 8.72 us -> none  [on_device(): squares = lax.all_to_all(squares, (Y, X, C), 0, 0, tiled=True)]
    all_to_all x4, blocking collectives: 120 us -> 115 us  [the longest x1 48.3 us: on_device(): lax.all_to_all(partial.reshape(NY * NZM, NZH, 8, COLS_DEV), DP, 0, 0, axi...]
    ppermute x1 -> x0, waiting for transfers between devices: 2.76 us -> none  [on_device(): recv = lax.ppermute(send, ZL, [(0, 1), (1, 0)])]
    all_to_all x1 -> x0, waiting for transfers between devices: 2.2 us -> none  [on_device(): squares = lax.all_to_all(squares, (Y, X, C), 0, 0, tiled=True)]
    ppermute x1 -> x0, starting transfers between devices: 1.92 us -> none  [on_device(): recv = lax.ppermute(send, ZL, [(0, 1), (1, 0)])]
  transfers between devices with their start and end apart: 2 -> 0, of which waited for: 2 -> 0; matrix products, arithmetic and copies ran while one was open for 0% -> 0% of each run, Pallas kernels for 0% -> 0%
where the time goes in v5:
time: 139 us; the launch traced here: 137 us
  blocking collectives  131 us (94%)
  Pallas kernels  5.86 us (4%)
    all_to_all x1, blocking collectives, on_device(): lax.all_to_all(partial.reshape(NY * NZM, NZH, 8, COLS_DEV), DP, 0, 0, axi...  48.3 us
    all_to_all x1, blocking collectives, on_device(): terms = lax.all_to_all(rows, ZH, 0, 0, tiled=True)  33.9 us
    all_to_all x1, blocking collectives, on_device(): squares = lax.all_to_all(squares, (Y, ZM, ZL, X, C), 0, 0, tiled=True)  26 us
    all_gather x1, blocking collectives, on_device(): squares = lax.all_gather(squares, ZH)  15.9 us
    all_to_all x1, blocking collectives, on_device(): terms = lax.all_to_all(rows, ZL, 0, 0, tiled=True)  6.55 us
    pallas_call x1, Pallas kernels, on_device(): pl.pallas_call(grad_kernel, in_specs=[pl.BlockSpec(memory_space=pltpu.HBM...  4.48 us

profile of v5, /device:TPU:1, one launch (start us, length us, event | category | flops | bytes accessed | tf_op | source)
XLA Modules:
  0.0 136.6 jit_solution(7263182252555573876)
XLA Ops:
  0.0 4.5 %grad.1 = f32[4,2,8,8,1024]{4,3,2,1,0:T(8,128)S(1)} custom-call(bf16[1024,512]{1,0:T(8,128)(2,1)} %a_hbm.1, bf16[1024,1024]{1,0:T(8,128)(2,1)} %b_hbm.1, bf16[512,1024]{1,0:T(8,128)(2,1)} %l_hbm.1), custom_call_target="tpu_custom_call" | custom-call | tf_op jit(solution)/shard_map/grad/pallas_call | solution.py:109
  4.5 48.3 %all_to_all.20.s_ref = f32[8,8,8,1024]{3,2,1,0:T(8,128)S(1)} all-to-all(f32[8,8,8,1024]{3,2,1,0:T(8,128)S(1)} %bitcast.2), channel_id=1, replica_groups={{8,16,264,272,520,528,776,784},{32,24,288,280,544,536,800,792},{40,48,2..., dimensions={0} | all-to-all | bytes 4194304 | tf_op jit(solution)/shard_map/all_to_all | solution.py:123
  52.8 0.0 copy-start
  52.8 0.0 copy-start.1
  52.8 0.1 fold.1
  52.9 6.5 %all_to_all.21 = f32[2,8,4,1024]{3,2,1,0:T(4,128)S(1)} all-to-all(f32[2,8,4,1024]{3,2,1,0:T(4,128)S(1)} %fold.1), channel_id=1, replica_groups=mesh['dp_y'=4,'dp_zh'=8,'dp_zm'=2,'dp_zl'=2,'mp_x'=4,'mp_c'=2] {'dp_zl'}, dimensions={0} | all-to-all | bytes 524288 | tf_op jit(solution)/shard_map/all_to_all | solution.py:139
  59.4 0.1 reduce_sum.9
  59.5 33.9 %all_to_all.22.s_ref = f32[8,4,1024]{2,1,0:T(4,128)S(1)} all-to-all(f32[8,4,1024]{2,1,0:T(4,128)S(1)} %reduce_sum.9), channel_id=1, replica_groups=mesh['dp_y'=4,'dp_zh'=8,'dp_zm'=2,'dp_zl'=2,'mp_x'=4,'mp_c'=2] {'dp_zh'}, dimensions={0} | all-to-all | bytes 262144 | tf_op jit(solution)/shard_map/all_to_all | solution.py:141
  93.4 0.0 copy-done
  93.4 0.4 mix.1
  93.8 26.0 %all_to_all.23.s_ref = f32[128,1,128]{2,1,0:T(1,128)S(1)} all-to-all(f32[128,1,128]{2,1,0:T(1,128)S(1)} %get-tuple-element.7), channel_id=1, replica_groups=mesh['dp_y'=4,'dp_zh'=8,'dp_zm'=2,'dp_zl'=2,'mp_x'=4,'mp_c'=2] {'dp_y','..., dimensions={0} | all-to-all | bytes 131072 | tf_op jit(solution)/shard_map/all_to_all | solution.py:150
  119.8 0.1 relay.1
  119.9 15.9 %all-gather.1.s_ref = f32[8,1,128]{2,1,0:T(1,128)S(1)} all-gather(f32[1,1,128]{2,1,0:T(1,128)S(1)} %bitcast.3), channel_id=2, replica_groups=mesh['dp_y'=4,'dp_zh'=8,'dp_zm'=2,'dp_zl'=2,'mp_x'=4,'mp_c'=2] {'dp_zh'}, dimensions={0}, use_global_device_ids=true | all-gather | bytes 4608 | tf_op jit(solution)/shard_map/all_gather | solution.py:159
  135.9 0.0 copy-done.1
  135.9 0.7 update.1
Async XLA Ops:
  52.8 40.6 %copy-start = (bf16[512,1024]{1,0:T(8,128)(2,1)S(1)}, bf16[512,1024]{1,0:T(8,128)(2,1)}, u32[]{:S(2)}) copy-start(bf16[512,1024]{1,0:T(8,128)(2,1)} %r_ref.1) | copy-start | bytes 3145732
  52.8 83.1 %copy-start.1 = (f32[4,1024]{1,0:T(4,128)S(1)}, f32[4,1024]{1,0:T(4,128)}, u32[]{:S(2)}) copy-start(f32[4,1024]{1,0:T(4,128)} %m_ref.1) | copy-start | bytes 49156

commit v6 on v5

--- a/solution.py
+++ b/solution.py
@@ -18,6 +18,19 @@
     for k in range(16)
 ]
 ENTRIES = 512 * 8192
+
+
+def rank(y, z, x, c):
+    return ((y * 32 + z) * NX + x) * NC + c
+
+
+GATHERS = [
+    [rank(y, r + 4 * q, x, 1) for q in range(8)] for y in range(4) for x in range(4) for r in range(4)
+] + [
+    [rank(y, z + (i ^ y) % 2, x, 0) for y in range(4) for i in range(2)]
+    for z in range(0, 32, 2)
+    for x in range(4)
+]
 
 clip_rms = 10.0
 step_size = 0.25
@@ -85,8 +98,9 @@
     o_ref[...] = jnp.sum(s_ref[...], axis=0)
 
 
-def update_kernel(s_ref, m_ref, p_ref, o_ref):
-    squares = jnp.sum(jnp.sum(s_ref[...], axis=0), axis=1, keepdims=True)
+def update_kernel(s_ref, t_ref, m_ref, p_ref, o_ref):
+    squares = jnp.where(lax.axis_index(C) == 1, s_ref[...], t_ref[...])
+    squares = jnp.sum(jnp.sum(squares, axis=0), axis=1, keepdims=True)
     root_mean = jnp.sqrt(squares / jnp.float32(ENTRIES) + epsilon)
     factor = jnp.minimum(jnp.float32(1.0), clip_rms / root_mean)
     scale = step_size * factor
@@ -156,15 +170,16 @@
         compiler_params=params(4),
         name="relay",
     )(squares)
-    squares = lax.all_gather(squares, ZH)
+    squares = lax.all_gather(squares, DP + MP, axis_index_groups=GATHERS)
+    across = lax.ppermute(squares, C, [(1, 0)])
     return pl.pallas_call(
         update_kernel,
-        in_specs=whole(3),
+        in_specs=whole(4),
         out_specs=pl.BlockSpec(memory_space=VMEM),
         out_shape=f32(4, COLS_DEV),
         compiler_params=params(4),
         name="update",
-    )(squares, master, precond)
+    )(squares, across, master, precond)
 
 
 def solution(mesh):

time: 139 us -> 139 us (level); the launches traced: 137 us -> 139 us
  transfers between devices with their start and end apart: 0 -> 1, of which waited for: 0 -> 1; matrix products, arithmetic and copies ran while one was open for 0% -> 0% of each run, Pallas kernels for 0% -> 0%
where the time goes in v6:
time: 139 us
  blocking collectives  131 us (94%)
  Pallas kernels  5.86 us (4%)
    all_to_all x1, blocking collectives, on_device(): lax.all_to_all(partial.reshape(NY * NZM, NZH, 8, COLS_DEV), DP, 0, 0, axi...  48.3 us
    all_to_all x1, blocking collectives, on_device(): terms = lax.all_to_all(rows, ZH, 0, 0, tiled=True)  33.9 us
    all_to_all x1, blocking collectives, on_device(): squares = lax.all_to_all(squares, (Y, ZM, ZL, X, C), 0, 0, tiled=True)  26 us
    all_gather x1, blocking collectives, on_device(): squares = lax.all_gather(squares, DP + MP, axis_index_groups=GATHERS)  15.9 us
    all_to_all x1, blocking collectives, on_device(): terms = lax.all_to_all(rows, ZL, 0, 0, tiled=True)  6.55 us
    pallas_call x1, Pallas kernels, on_device(): pl.pallas_call(grad_kernel, in_specs=[pl.BlockSpec(memory_space=pltpu.HBM...  4.48 us
  transfers between devices with their start and end apart: 1, of which 1 were waited for; matrix products, arithmetic and copies ran while one was open for 0% of the time, Pallas kernels for 0%

profile of v6, /device:TPU:1, one launch (start us, length us, event | category | flops | bytes accessed | tf_op | source)
XLA Modules:
  0.0 138.7 jit_solution(353185021156603664)
XLA Ops:
  0.0 4.5 %grad.1 = f32[4,2,8,8,1024]{4,3,2,1,0:T(8,128)S(1)} custom-call(bf16[1024,512]{1,0:T(8,128)(2,1)} %a_hbm.1, bf16[1024,1024]{1,0:T(8,128)(2,1)} %b_hbm.1, bf16[512,1024]{1,0:T(8,128)(2,1)} %l_hbm.1), custom_call_target="tpu_custom_call" | custom-call | tf_op jit(solution)/shard_map/grad/pallas_call | solution.py:123
  4.5 48.3 %all_to_all.20.s_ref = f32[8,8,8,1024]{3,2,1,0:T(8,128)S(1)} all-to-all(f32[8,8,8,1024]{3,2,1,0:T(8,128)S(1)} %bitcast.2), channel_id=1, replica_groups={{8,16,264,272,520,528,776,784},{32,24,288,280,544,536,800,792},{40,48,2..., dimensions={0} | all-to-all | bytes 4194304 | tf_op jit(solution)/shard_map/all_to_all | solution.py:137
  52.8 0.0 copy-start
  52.8 0.0 copy-start.1
  52.8 0.1 fold.1
  52.9 6.5 %all_to_all.21 = f32[2,8,4,1024]{3,2,1,0:T(4,128)S(1)} all-to-all(f32[2,8,4,1024]{3,2,1,0:T(4,128)S(1)} %fold.1), channel_id=1, replica_groups=mesh['dp_y'=4,'dp_zh'=8,'dp_zm'=2,'dp_zl'=2,'mp_x'=4,'mp_c'=2] {'dp_zl'}, dimensions={0} | all-to-all | bytes 524288 | tf_op jit(solution)/shard_map/all_to_all | solution.py:153
  59.4 0.1 reduce_sum.9
  59.5 33.9 %all_to_all.22.s_ref = f32[8,4,1024]{2,1,0:T(4,128)S(1)} all-to-all(f32[8,4,1024]{2,1,0:T(4,128)S(1)} %reduce_sum.9), channel_id=1, replica_groups=mesh['dp_y'=4,'dp_zh'=8,'dp_zm'=2,'dp_zl'=2,'mp_x'=4,'mp_c'=2] {'dp_zh'}, dimensions={0} | all-to-all | bytes 262144 | tf_op jit(solution)/shard_map/all_to_all | solution.py:155
  93.4 0.0 copy-done
  93.4 0.4 mix.1
  93.8 26.0 %all_to_all.23.s_ref = f32[128,1,128]{2,1,0:T(1,128)S(1)} all-to-all(f32[128,1,128]{2,1,0:T(1,128)S(1)} %get-tuple-element.7), channel_id=1, replica_groups=mesh['dp_y'=4,'dp_zh'=8,'dp_zm'=2,'dp_zl'=2,'mp_x'=4,'mp_c'=2] {'dp_y','..., dimensions={0} | all-to-all | bytes 131072 | tf_op jit(solution)/shard_map/all_to_all | solution.py:164
  119.8 0.1 relay.1
  119.9 15.9 %all-gather.1.s_ref = f32[8,1,128]{2,1,0:T(1,128)S(1)} all-gather(f32[1,1,128]{2,1,0:T(1,128)S(1)} %bitcast.3), channel_id=2, replica_groups={{1,33,65,97,129,161,193,225},{9,41,73,105,137,169,201,233},{17,49,81,11..., dimensions={0}, use_global_device_ids=true | all-gather | bytes 4608 | tf_op jit(solution)/shard_map/all_gather | solution.py:173
  135.9 1.3 collective-permute-start
  137.1 0.8 collective-permute-done.t_ref
  137.9 0.0 copy-done.1
  138.0 0.7 update.1
Async XLA Ops:
  52.8 40.6 %copy-start = (bf16[512,1024]{1,0:T(8,128)(2,1)S(1)}, bf16[512,1024]{1,0:T(8,128)(2,1)}, u32[]{:S(2)}) copy-start(bf16[512,1024]{1,0:T(8,128)(2,1)} %r_ref.1) | copy-start | bytes 3145732
  52.8 85.2 %copy-start.1 = (f32[4,1024]{1,0:T(4,128)S(1)}, f32[4,1024]{1,0:T(4,128)}, u32[]{:S(2)}) copy-start(f32[4,1024]{1,0:T(4,128)} %m_ref.1) | copy-start | bytes 49156
  135.9 2.1 %collective-permute-start = (f32[8,1,128]{2,1,0:T(1,128)S(1)}, f32[8,1,128]{2,1,0:T(1,128)S(1)}, u32[]{:S(2)}, u32[]{:S(2)}) collective-permute-start(f32[8,1,128]{2,1,0:T(1,128)S(1)} %all-gather.1.s_ref), channel_id=1, source_target_pairs={{1,0},{3,2},{5,4},{7,6},{9,8},{11,10},{13,12},{15,14},{17,16},{19,... | collective-permute-start | bytes 12296 | tf_op jit(solution)/shard_map/ppermute | solution.py:174

commit v7 on v6

--- a/solution.py
+++ b/solution.py
@@ -13,8 +13,20 @@
 NY, NZH, NZM, NZL, NX, NC = 4, 8, 2, 2, 4, 2
 ROWS, COLS_DEV = 512, 1024
 PEERS = NY * NZM * NZL * NX * NC
-NEIGHBOURS = [
-    [y * 32 + z % 32 for y in range(4) for z in ((2 * k + 1, 2 * k + 2) if k % 2 == 0 else (2 * k + 2, 2 * k + 1))]
+def gray(z):
+    return (z ^ z >> 1) & 1
+
+
+def bit1(z):
+    return z >> 1 & 1
+
+
+FIRST = [
+    [y * 32 + z for y in range(NY) for z in sorted((2 * j, 2 * j + 1), key=gray)] for j in range(16)
+]
+SECOND = [
+    [y * 32 + z for z in sorted((2 * k + 1, (2 * k + 2) % 32), key=bit1)]
+    for y in range(NY)
     for k in range(16)
 ]
 ENTRIES = 512 * 8192
@@ -69,14 +81,18 @@
         left = l_ref[c]
         p = dot(left, hi) + dot(left, lo)
         p = p.reshape(NY, NZH, NZM, 8, BLOCK)
-        for m in range(NZM):
-            o_ref[:, m, :, :, pl.ds(c * BLOCK, BLOCK)] = p[:, :, m]
+        even, odd = p[:, :, 0], p[:, :, 1]
+        upper = lax.broadcasted_iota(jnp.int32, even.shape, 2) < 4
+        cols = pl.ds(c * BLOCK, BLOCK)
+        o_ref[:, 0, :, :, cols] = jnp.where(upper, even, odd)
+        o_ref[:, 1, :, :, cols] = jnp.where(upper, odd, even)
 
 
 def fold_kernel(s_ref, o_ref):
     rows = jnp.sum(s_ref[...], axis=0)
-    o_ref[0] = rows[:, :4]
-    o_ref[1] = rows[:, 4:]
+    same = lax.axis_index(ZM) == lax.axis_index(ZL)
+    o_ref[0] = jnp.where(same, rows[:, :4], rows[:, 4:])
+    o_ref[1] = jnp.where(same, rows[:, 4:], rows[:, :4])
 
 
 def mix_kernel(s_ref, r_ref, p_ref, ss_ref):
@@ -124,7 +140,7 @@
         grad_kernel,
         in_specs=[pl.BlockSpec(memory_space=pltpu.HBM)] * 3,
         out_specs=pl.BlockSpec(memory_space=VMEM),
-        out_shape=VMEM((NY, NZM, NZH, 8, COLS_DEV), jnp.float32),
+        out_shape=VMEM((NY, 2, NZH, 8, COLS_DEV), jnp.float32),
         scratch_shapes=[
             VMEM((1024, ROWS), jnp.bfloat16),
             VMEM((2, 1024, BLOCK), jnp.bfloat16),
@@ -135,22 +151,22 @@
         name="grad",
     )(tokens_in, out_grad, left_root)
     terms = lax.all_to_all(
-        partial.reshape(NY * NZM, NZH, 8, COLS_DEV),
+        partial.reshape(NY * 2, NZH, 8, COLS_DEV),
         DP,
         0,
         0,
-        axis_index_groups=NEIGHBOURS,
+        axis_index_groups=FIRST,
         tiled=True,
     )
     rows = pl.pallas_call(
         fold_kernel,
         in_specs=whole(1),
         out_specs=pl.BlockSpec(memory_space=VMEM),
-        out_shape=VMEM((NZL, NZH, 4, COLS_DEV), jnp.float32),
+        out_shape=VMEM((NZM, NZH, 4, COLS_DEV), jnp.float32),
         compiler_params=params(8),
         name="fold",
     )(terms)
-    terms = lax.all_to_all(rows, ZL, 0, 0, tiled=True)
+    terms = lax.all_to_all(rows, DP, 0, 0, axis_index_groups=SECOND, tiled=True)
     rows = jnp.sum(terms, axis=0)
     terms = lax.all_to_all(rows, ZH, 0, 0, tiled=True)
     precond, squares = pl.pallas_call(

time: 139 us -> 139 us (level)
    all_to_all x1, blocking collectives: 26 us -> 21 us  [on_device(): squares = lax.all_to_all(squares, (Y, ZM, ZL, X, C), 0, 0, tiled=True)]
    all_to_all x1, blocking collectives: 33.9 us -> 37.8 us  [on_device(): terms = lax.all_to_all(rows, ZH, 0, 0, tiled=True)]
where the time goes in v7:
time: 139 us
  blocking collectives  131 us (94%)
  Pallas kernels  5.86 us (4%)
    all_to_all x1, blocking collectives, on_device(): terms = lax.all_to_all(rows, ZH, 0, 0, tiled=True)  37.8 us
    all_to_all x1, blocking collectives, on_device(): terms = lax.all_to_all(rows, DP, 0, 0, axis_index_groups=SECOND, tiled=True)  32 us
    all_to_all x1, blocking collectives, on_device(): lax.all_to_all(partial.reshape(NY * 2, NZH, 8, COLS_DEV), DP, 0, 0, axis_...  22.6 us
    all_to_all x1, blocking collectives, on_device(): squares = lax.all_to_all(squares, (Y, ZM, ZL, X, C), 0, 0, tiled=True)  21 us
    all_gather x1, blocking collectives, on_device(): squares = lax.all_gather(squares, DP + MP, axis_index_groups=GATHERS)  17.1 us
    pallas_call x1, Pallas kernels, on_device(): pl.pallas_call(grad_kernel, in_specs=[pl.BlockSpec(memory_space=pltpu.HBM...  4.48 us
  transfers between devices with their start and end apart: 1, of which 1 were waited for; matrix products, arithmetic and copies ran while one was open for 0% of the time, Pallas kernels for 0%

profile of v7, /device:TPU:1, one launch (start us, length us, event | category | flops | bytes accessed | tf_op | source)
XLA Modules:
  0.0 138.6 jit_solution(782150006359820759)
XLA Ops:
  0.0 4.5 %grad.1 = f32[4,2,8,8,1024]{4,3,2,1,0:T(8,128)S(1)} custom-call(bf16[1024,512]{1,0:T(8,128)(2,1)} %a_hbm.1, bf16[1024,1024]{1,0:T(8,128)(2,1)} %b_hbm.1, bf16[512,1024]{1,0:T(8,128)(2,1)} %l_hbm.1), custom_call_target="tpu_custom_call" | custom-call | tf_op jit(solution)/shard_map/grad/pallas_call | solution.py:139
  4.5 22.6 %all_to_all.20.s_ref = f32[8,8,8,1024]{3,2,1,0:T(8,128)S(1)} all-to-all(f32[8,8,8,1024]{3,2,1,0:T(8,128)S(1)} %bitcast.2), channel_id=1, replica_groups={{0,8,256,264,512,520,768,776},{24,16,280,272,536,528,792,784},{32,40,28..., dimensions={0} | all-to-all | bytes 4194304 | tf_op jit(solution)/shard_map/all_to_all | solution.py:153
  27.1 0.0 copy-start
  27.1 0.0 copy-start.1
  27.1 0.1 fold.1
  27.2 32.0 %all_to_all.21 = f32[2,8,4,1024]{3,2,1,0:T(4,128)S(1)} all-to-all(f32[2,8,4,1024]{3,2,1,0:T(4,128)S(1)} %fold.1), channel_id=1, replica_groups={{8,16},{32,24},{40,48},{64,56},{72,80},{96,88},{104,112},{128,120},{136..., dimensions={0} | all-to-all | bytes 524288 | tf_op jit(solution)/shard_map/all_to_all | solution.py:169
  59.2 0.1 reduce_sum.9
  59.2 37.8 %all_to_all.22.s_ref = f32[8,4,1024]{2,1,0:T(4,128)S(1)} all-to-all(f32[8,4,1024]{2,1,0:T(4,128)S(1)} %reduce_sum.9), channel_id=1, replica_groups=mesh['dp_y'=4,'dp_zh'=8,'dp_zm'=2,'dp_zl'=2,'mp_x'=4,'mp_c'=2] {'dp_zh'}, dimensions={0} | all-to-all | bytes 262144 | tf_op jit(solution)/shard_map/all_to_all | solution.py:171
  97.0 0.0 copy-done
  97.0 0.4 mix.1
  97.5 21.0 %all_to_all.23.s_ref = f32[128,1,128]{2,1,0:T(1,128)S(1)} all-to-all(f32[128,1,128]{2,1,0:T(1,128)S(1)} %get-tuple-element.7), channel_id=1, replica_groups=mesh['dp_y'=4,'dp_zh'=8,'dp_zm'=2,'dp_zl'=2,'mp_x'=4,'mp_c'=2] {'dp_y','..., dimensions={0} | all-to-all | bytes 131072 | tf_op jit(solution)/shard_map/all_to_all | solution.py:180
  118.5 0.1 relay.1
  118.6 17.1 %all-gather.1.s_ref = f32[8,1,128]{2,1,0:T(1,128)S(1)} all-gather(f32[1,1,128]{2,1,0:T(1,128)S(1)} %bitcast.3), channel_id=2, replica_groups={{1,33,65,97,129,161,193,225},{9,41,73,105,137,169,201,233},{17,49,81,11..., dimensions={0}, use_global_device_ids=true | all-gather | bytes 4608 | tf_op jit(solution)/shard_map/all_gather | solution.py:189
  135.8 1.3 collective-permute-start
  137.1 0.8 collective-permute-done.t_ref
  137.9 0.0 copy-done.1
  137.9 0.7 update.1
Async XLA Ops:
  27.1 70.0 %copy-start = (bf16[512,1024]{1,0:T(8,128)(2,1)S(1)}, bf16[512,1024]{1,0:T(8,128)(2,1)}, u32[]{:S(2)}) copy-start(bf16[512,1024]{1,0:T(8,128)(2,1)} %r_ref.1) | copy-start | bytes 3145732
  27.1 110.8 %copy-start.1 = (f32[4,1024]{1,0:T(4,128)S(1)}, f32[4,1024]{1,0:T(4,128)}, u32[]{:S(2)}) copy-start(f32[4,1024]{1,0:T(4,128)} %m_ref.1) | copy-start | bytes 49156
  135.8 2.1 %collective-permute-start = (f32[8,1,128]{2,1,0:T(1,128)S(1)}, f32[8,1,128]{2,1,0:T(1,128)S(1)}, u32[]{:S(2)}, u32[]{:S(2)}) collective-permute-start(f32[8,1,128]{2,1,0:T(1,128)S(1)} %all-gather.1.s_ref), channel_id=1, source_target_pairs={{1,0},{3,2},{5,4},{7,6},{9,8},{11,10},{13,12},{15,14},{17,16},{19,... | collective-permute-start | bytes 12296 | tf_op jit(solution)/shard_map/ppermute | solution.py:190

commit v8 on v7

--- a/solution.py
+++ b/solution.py
@@ -30,6 +30,7 @@
     for k in range(16)
 ]
 ENTRIES = 512 * 8192
+LEAD_NS = 8000
 
 
 def rank(y, z, x, c):
@@ -87,6 +88,10 @@
         o_ref[:, 0, :, :, cols] = jnp.where(upper, even, odd)
         o_ref[:, 1, :, :, cols] = jnp.where(upper, odd, even)
 
+    @pl.when(lax.axis_index(C) == 1)
+    def _():
+        pl.delay(LEAD_NS)
+
 
 def fold_kernel(s_ref, o_ref):
     rows = jnp.sum(s_ref[...], axis=0)

time: 139 us -> 136 us (0.978)
  blocking collectives: 131 us -> 120 us
  Pallas kernels: 5.86 us -> 13.9 us
    all_to_all x1, blocking collectives: 32 us -> 17.7 us  [on_device(): terms = lax.all_to_all(rows, DP, 0, 0, axis_index_groups=SECOND, tiled=True)]
    all_to_all x1, blocking collectives: 22.6 us -> 31.1 us  [on_device(): lax.all_to_all(partial.reshape(NY * 2, NZH, 8, COLS_DEV), DP, 0, 0, axis_...]
    pallas_call x1, Pallas kernels: 4.48 us -> 12.5 us  [on_device(): pl.pallas_call(grad_kernel, in_specs=[pl.BlockSpec(memory_space=pltpu.HBM...]
    all_to_all x1, blocking collectives: 21 us -> 16.7 us  [on_device(): squares = lax.all_to_all(squares, (Y, ZM, ZL, X, C), 0, 0, tiled=True)]
where the time goes in v8:
time: 136 us
  blocking collectives  120 us (88%)
  Pallas kernels  13.9 us (10%)
    all_to_all x1, blocking collectives, on_device(): terms = lax.all_to_all(rows, ZH, 0, 0, tiled=True)  37.6 us
    all_to_all x1, blocking collectives, on_device(): lax.all_to_all(partial.reshape(NY * 2, NZH, 8, COLS_DEV), DP, 0, 0, axis_...  31.1 us
    all_to_all x1, blocking collectives, on_device(): terms = lax.all_to_all(rows, DP, 0, 0, axis_index_groups=SECOND, tiled=True)  17.7 us
    all_gather x1, blocking collectives, on_device(): squares = lax.all_gather(squares, DP + MP, axis_index_groups=GATHERS)  16.8 us
    all_to_all x1, blocking collectives, on_device(): squares = lax.all_to_all(squares, (Y, ZM, ZL, X, C), 0, 0, tiled=True)  16.7 us
    pallas_call x1, Pallas kernels, on_device(): pl.pallas_call(grad_kernel, in_specs=[pl.BlockSpec(memory_space=pltpu.HBM...  12.5 us
  transfers between devices with their start and end apart: 1, of which 1 were waited for; matrix products, arithmetic and copies ran while one was open for 0% of the time, Pallas kernels for 0%

profile of v8, /device:TPU:1, one launch (start us, length us, event | category | flops | bytes accessed | tf_op | source)
XLA Modules:
  0.0 136.1 jit_solution(17981908936964617718)
XLA Ops:
  0.0 12.5 %grad.1 = f32[4,2,8,8,1024]{4,3,2,1,0:T(8,128)S(1)} custom-call(bf16[1024,512]{1,0:T(8,128)(2,1)} %a_hbm.1, bf16[1024,1024]{1,0:T(8,128)(2,1)} %b_hbm.1, bf16[512,1024]{1,0:T(8,128)(2,1)} %l_hbm.1), custom_call_target="tpu_custom_call" | custom-call | tf_op jit(solution)/shard_map/grad/pallas_call | solution.py:144
  12.5 31.1 %all_to_all.20.s_ref = f32[8,8,8,1024]{3,2,1,0:T(8,128)S(1)} all-to-all(f32[8,8,8,1024]{3,2,1,0:T(8,128)S(1)} %bitcast.2), channel_id=1, replica_groups={{0,8,256,264,512,520,768,776},{24,16,280,272,536,528,792,784},{32,40,28..., dimensions={0} | all-to-all | bytes 4194304 | tf_op jit(solution)/shard_map/all_to_all | solution.py:158
  43.5 0.0 copy-start
  43.6 0.0 copy-start.1
  43.6 0.1 fold.1
  43.7 17.7 %all_to_all.21 = f32[2,8,4,1024]{3,2,1,0:T(4,128)S(1)} all-to-all(f32[2,8,4,1024]{3,2,1,0:T(4,128)S(1)} %fold.1), channel_id=1, replica_groups={{8,16},{32,24},{40,48},{64,56},{72,80},{96,88},{104,112},{128,120},{136..., dimensions={0} | all-to-all | bytes 524288 | tf_op jit(solution)/shard_map/all_to_all | solution.py:174
  61.4 0.1 reduce_sum.9
  61.5 37.6 %all_to_all.22.s_ref = f32[8,4,1024]{2,1,0:T(4,128)S(1)} all-to-all(f32[8,4,1024]{2,1,0:T(4,128)S(1)} %reduce_sum.9), channel_id=1, replica_groups=mesh['dp_y'=4,'dp_zh'=8,'dp_zm'=2,'dp_zl'=2,'mp_x'=4,'mp_c'=2] {'dp_zh'}, dimensions={0} | all-to-all | bytes 262144 | tf_op jit(solution)/shard_map/all_to_all | solution.py:176
  99.1 0.0 copy-done
  99.1 0.4 mix.1
  99.5 16.7 %all_to_all.23.s_ref = f32[128,1,128]{2,1,0:T(1,128)S(1)} all-to-all(f32[128,1,128]{2,1,0:T(1,128)S(1)} %get-tuple-element.7), channel_id=1, replica_groups=mesh['dp_y'=4,'dp_zh'=8,'dp_zm'=2,'dp_zl'=2,'mp_x'=4,'mp_c'=2] {'dp_y','..., dimensions={0} | all-to-all | bytes 131072 | tf_op jit(solution)/shard_map/all_to_all | solution.py:185
  116.3 0.1 relay.1
  116.4 16.8 %all-gather.1.s_ref = f32[8,1,128]{2,1,0:T(1,128)S(1)} all-gather(f32[1,1,128]{2,1,0:T(1,128)S(1)} %bitcast.3), channel_id=2, replica_groups={{1,33,65,97,129,161,193,225},{9,41,73,105,137,169,201,233},{17,49,81,11..., dimensions={0}, use_global_device_ids=true | all-gather | bytes 4608 | tf_op jit(solution)/shard_map/all_gather | solution.py:194
  133.2 1.3 collective-permute-start
  134.5 0.8 collective-permute-done.t_ref
  135.3 0.0 copy-done.1
  135.3 0.7 update.1
Async XLA Ops:
  43.5 55.6 %copy-start = (bf16[512,1024]{1,0:T(8,128)(2,1)S(1)}, bf16[512,1024]{1,0:T(8,128)(2,1)}, u32[]{:S(2)}) copy-start(bf16[512,1024]{1,0:T(8,128)(2,1)} %r_ref.1) | copy-start | bytes 3145732
  43.6 91.8 %copy-start.1 = (f32[4,1024]{1,0:T(4,128)S(1)}, f32[4,1024]{1,0:T(4,128)}, u32[]{:S(2)}) copy-start(f32[4,1024]{1,0:T(4,128)} %m_ref.1) | copy-start | bytes 49156
  133.2 2.1 %collective-permute-start = (f32[8,1,128]{2,1,0:T(1,128)S(1)}, f32[8,1,128]{2,1,0:T(1,128)S(1)}, u32[]{:S(2)}, u32[]{:S(2)}) collective-permute-start(f32[8,1,128]{2,1,0:T(1,128)S(1)} %all-gather.1.s_ref), channel_id=1, source_target_pairs={{1,0},{3,2},{5,4},{7,6},{9,8},{11,10},{13,12},{15,14},{17,16},{19,... | collective-permute-start | bytes 12296 | tf_op jit(solution)/shard_map/ppermute | solution.py:195

commit v9 on v8

--- a/solution.py
+++ b/solution.py
@@ -30,7 +30,7 @@
     for k in range(16)
 ]
 ENTRIES = 512 * 8192
-LEAD_NS = 8000
+LEAD_NS = 5500
 
 
 def rank(y, z, x, c):

time: 136 us -> 139 us (1.022)
  blocking collectives: 120 us -> 125 us
  Pallas kernels: 13.9 us -> 11.4 us
    all_to_all x1, blocking collectives: 17.7 us -> 23.5 us  [on_device(): terms = lax.all_to_all(rows, DP, 0, 0, axis_index_groups=SECOND, tiled=True)]
    all_to_all x1, blocking collectives: 31.1 us -> 28 us  [on_device(): lax.all_to_all(partial.reshape(NY * 2, NZH, 8, COLS_DEV), DP, 0, 0, axis_...]
    pallas_call x1, Pallas kernels: 12.5 us -> 9.98 us  [on_device(): pl.pallas_call(grad_kernel, in_specs=[pl.BlockSpec(memory_space=pltpu.HBM...]
    all_to_all x1, blocking collectives: 37.6 us -> 39.9 us  [on_device(): terms = lax.all_to_all(rows, ZH, 0, 0, tiled=True)]
where the time goes in v9:
time: 139 us
  blocking collectives  125 us (90%)
  Pallas kernels  11.4 us (8%)
    all_to_all x1, blocking collectives, on_device(): terms = lax.all_to_all(rows, ZH, 0, 0, tiled=True)  39.9 us
    all_to_all x1, blocking collectives, on_device(): lax.all_to_all(partial.reshape(NY * 2, NZH, 8, COLS_DEV), DP, 0, 0, axis_...  28 us
    all_to_all x1, blocking collectives, on_device(): terms = lax.all_to_all(rows, DP, 0, 0, axis_index_groups=SECOND, tiled=True)  23.5 us
    all_gather x1, blocking collectives, on_device(): squares = lax.all_gather(squares, DP + MP, axis_index_groups=GATHERS)  17.5 us
    all_to_all x1, blocking collectives, on_device(): squares = lax.all_to_all(squares, (Y, ZM, ZL, X, C), 0, 0, tiled=True)  16.2 us
    pallas_call x1, Pallas kernels, on_device(): pl.pallas_call(grad_kernel, in_specs=[pl.BlockSpec(memory_space=pltpu.HBM...  9.98 us
  transfers between devices with their start and end apart: 1, of which 1 were waited for; matrix products, arithmetic and copies ran while one was open for 0% of the time, Pallas kernels for 0%

profile of v9, /device:TPU:1, one launch (start us, length us, event | category | flops | bytes accessed | tf_op | source)
XLA Modules:
  0.0 138.6 jit_solution(14478194910643490259)
XLA Ops:
  0.0 10.0 %grad.1 = f32[4,2,8,8,1024]{4,3,2,1,0:T(8,128)S(1)} custom-call(bf16[1024,512]{1,0:T(8,128)(2,1)} %a_hbm.1, bf16[1024,1024]{1,0:T(8,128)(2,1)} %b_hbm.1, bf16[512,1024]{1,0:T(8,128)(2,1)} %l_hbm.1), custom_call_target="tpu_custom_call" | custom-call | tf_op jit(solution)/shard_map/grad/pallas_call | solution.py:144
  10.0 28.0 %all_to_all.20.s_ref = f32[8,8,8,1024]{3,2,1,0:T(8,128)S(1)} all-to-all(f32[8,8,8,1024]{3,2,1,0:T(8,128)S(1)} %bitcast.2), channel_id=1, replica_groups={{0,8,256,264,512,520,768,776},{24,16,280,272,536,528,792,784},{32,40,28..., dimensions={0} | all-to-all | bytes 4194304 | tf_op jit(solution)/shard_map/all_to_all | solution.py:158
  38.0 0.0 copy-start
  38.0 0.0 copy-start.1
  38.0 0.1 fold.1
  38.1 23.5 %all_to_all.21 = f32[2,8,4,1024]{3,2,1,0:T(4,128)S(1)} all-to-all(f32[2,8,4,1024]{3,2,1,0:T(4,128)S(1)} %fold.1), channel_id=1, replica_groups={{8,16},{32,24},{40,48},{64,56},{72,80},{96,88},{104,112},{128,120},{136..., dimensions={0} | all-to-all | bytes 524288 | tf_op jit(solution)/shard_map/all_to_all | solution.py:174
  61.6 0.1 reduce_sum.9
  61.7 39.9 %all_to_all.22.s_ref = f32[8,4,1024]{2,1,0:T(4,128)S(1)} all-to-all(f32[8,4,1024]{2,1,0:T(4,128)S(1)} %reduce_sum.9), channel_id=1, replica_groups=mesh['dp_y'=4,'dp_zh'=8,'dp_zm'=2,'dp_zl'=2,'mp_x'=4,'mp_c'=2] {'dp_zh'}, dimensions={0} | all-to-all | bytes 262144 | tf_op jit(solution)/shard_map/all_to_all | solution.py:176
  101.6 0.0 copy-done
  101.6 0.4 mix.1
  102.0 16.2 %all_to_all.23.s_ref = f32[128,1,128]{2,1,0:T(1,128)S(1)} all-to-all(f32[128,1,128]{2,1,0:T(1,128)S(1)} %get-tuple-element.7), channel_id=1, replica_groups=mesh['dp_y'=4,'dp_zh'=8,'dp_zm'=2,'dp_zl'=2,'mp_x'=4,'mp_c'=2] {'dp_y','..., dimensions={0} | all-to-all | bytes 131072 | tf_op jit(solution)/shard_map/all_to_all | solution.py:185
  118.2 0.1 relay.1
  118.3 17.5 %all-gather.1.s_ref = f32[8,1,128]{2,1,0:T(1,128)S(1)} all-gather(f32[1,1,128]{2,1,0:T(1,128)S(1)} %bitcast.3), channel_id=2, replica_groups={{1,33,65,97,129,161,193,225},{9,41,73,105,137,169,201,233},{17,49,81,11..., dimensions={0}, use_global_device_ids=true | all-gather | bytes 4608 | tf_op jit(solution)/shard_map/all_gather | solution.py:194
  135.8 1.3 collective-permute-start
  137.1 0.8 collective-permute-done.t_ref
  137.9 0.0 copy-done.1
  137.9 0.7 update.1
Async XLA Ops:
  38.0 63.6 %copy-start = (bf16[512,1024]{1,0:T(8,128)(2,1)S(1)}, bf16[512,1024]{1,0:T(8,128)(2,1)}, u32[]{:S(2)}) copy-start(bf16[512,1024]{1,0:T(8,128)(2,1)} %r_ref.1) | copy-start | bytes 3145732
  38.0 99.9 %copy-start.1 = (f32[4,1024]{1,0:T(4,128)S(1)}, f32[4,1024]{1,0:T(4,128)}, u32[]{:S(2)}) copy-start(f32[4,1024]{1,0:T(4,128)} %m_ref.1) | copy-start | bytes 49156
  135.8 2.1 %collective-permute-start = (f32[8,1,128]{2,1,0:T(1,128)S(1)}, f32[8,1,128]{2,1,0:T(1,128)S(1)}, u32[]{:S(2)}, u32[]{:S(2)}) collective-permute-start(f32[8,1,128]{2,1,0:T(1,128)S(1)} %all-gather.1.s_ref), channel_id=1, source_target_pairs={{1,0},{3,2},{5,4},{7,6},{9,8},{11,10},{13,12},{15,14},{17,16},{19,... | collective-permute-start | bytes 12296 | tf_op jit(solution)/shard_map/ppermute | solution.py:195

commit v10 on v9

--- a/solution.py
+++ b/solution.py
@@ -30,7 +30,7 @@
     for k in range(16)
 ]
 ENTRIES = 512 * 8192
-LEAD_NS = 5500
+LEAD_NS = 9500
 
 
 def rank(y, z, x, c):

time: 139 us -> 136 us (0.978)
  blocking collectives: 125 us -> 118 us
  Pallas kernels: 11.4 us -> 15.4 us
    all_to_all x1, blocking collectives: 23.5 us -> 14.8 us  [on_device(): terms = lax.all_to_all(rows, DP, 0, 0, axis_index_groups=SECOND, tiled=True)]
    all_to_all x1, blocking collectives: 28 us -> 32.5 us  [on_device(): lax.all_to_all(partial.reshape(NY * 2, NZH, 8, COLS_DEV), DP, 0, 0, axis_...]
    pallas_call x1, Pallas kernels: 9.98 us -> 14 us  [on_device(): pl.pallas_call(grad_kernel, in_specs=[pl.BlockSpec(memory_space=pltpu.HBM...]
    all_to_all x1, blocking collectives: 39.9 us -> 35.9 us  [on_device(): terms = lax.all_to_all(rows, ZH, 0, 0, tiled=True)]
where the time goes in v10:
time: 136 us
  blocking collectives  118 us (87%)
  Pallas kernels  15.4 us (11%)
    all_to_all x1, blocking collectives, on_device(): terms = lax.all_to_all(rows, ZH, 0, 0, tiled=True)  35.9 us
    all_to_all x1, blocking collectives, on_device(): lax.all_to_all(partial.reshape(NY * 2, NZH, 8, COLS_DEV), DP, 0, 0, axis_...  32.5 us
    all_gather x1, blocking collectives, on_device(): squares = lax.all_gather(squares, DP + MP, axis_index_groups=GATHERS)  17.8 us
    all_to_all x1, blocking collectives, on_device(): squares = lax.all_to_all(squares, (Y, ZM, ZL, X, C), 0, 0, tiled=True)  17.5 us
    all_to_all x1, blocking collectives, on_device(): terms = lax.all_to_all(rows, DP, 0, 0, axis_index_groups=SECOND, tiled=True)  14.8 us
    pallas_call x1, Pallas kernels, on_device(): pl.pallas_call(grad_kernel, in_specs=[pl.BlockSpec(memory_space=pltpu.HBM...  14 us
  transfers between devices with their start and end apart: 1, of which 1 were waited for; matrix products, arithmetic and copies ran while one was open for 0% of the time, Pallas kernels for 0%

profile of v10, /device:TPU:1, one launch (start us, length us, event | category | flops | bytes accessed | tf_op | source)
XLA Modules:
  0.0 136.1 jit_solution(3417919376625546940)
XLA Ops:
  0.0 14.0 %grad.1 = f32[4,2,8,8,1024]{4,3,2,1,0:T(8,128)S(1)} custom-call(bf16[1024,512]{1,0:T(8,128)(2,1)} %a_hbm.1, bf16[1024,1024]{1,0:T(8,128)(2,1)} %b_hbm.1, bf16[512,1024]{1,0:T(8,128)(2,1)} %l_hbm.1), custom_call_target="tpu_custom_call" | custom-call | tf_op jit(solution)/shard_map/grad/pallas_call | solution.py:144
  14.0 32.5 %all_to_all.20.s_ref = f32[8,8,8,1024]{3,2,1,0:T(8,128)S(1)} all-to-all(f32[8,8,8,1024]{3,2,1,0:T(8,128)S(1)} %bitcast.2), channel_id=1, replica_groups={{0,8,256,264,512,520,768,776},{24,16,280,272,536,528,792,784},{32,40,28..., dimensions={0} | all-to-all | bytes 4194304 | tf_op jit(solution)/shard_map/all_to_all | solution.py:158
  46.5 0.0 copy-start
  46.5 0.0 copy-start.1
  46.5 0.1 fold.1
  46.6 14.8 %all_to_all.21 = f32[2,8,4,1024]{3,2,1,0:T(4,128)S(1)} all-to-all(f32[2,8,4,1024]{3,2,1,0:T(4,128)S(1)} %fold.1), channel_id=1, replica_groups={{8,16},{32,24},{40,48},{64,56},{72,80},{96,88},{104,112},{128,120},{136..., dimensions={0} | all-to-all | bytes 524288 | tf_op jit(solution)/shard_map/all_to_all | solution.py:174
  61.4 0.1 reduce_sum.9
  61.5 35.9 %all_to_all.22.s_ref = f32[8,4,1024]{2,1,0:T(4,128)S(1)} all-to-all(f32[8,4,1024]{2,1,0:T(4,128)S(1)} %reduce_sum.9), channel_id=1, replica_groups=mesh['dp_y'=4,'dp_zh'=8,'dp_zm'=2,'dp_zl'=2,'mp_x'=4,'mp_c'=2] {'dp_zh'}, dimensions={0} | all-to-all | bytes 262144 | tf_op jit(solution)/shard_map/all_to_all | solution.py:176
  97.4 0.0 copy-done
  97.4 0.4 mix.1
  97.8 17.5 %all_to_all.23.s_ref = f32[128,1,128]{2,1,0:T(1,128)S(1)} all-to-all(f32[128,1,128]{2,1,0:T(1,128)S(1)} %get-tuple-element.7), channel_id=1, replica_groups=mesh['dp_y'=4,'dp_zh'=8,'dp_zm'=2,'dp_zl'=2,'mp_x'=4,'mp_c'=2] {'dp_y','..., dimensions={0} | all-to-all | bytes 131072 | tf_op jit(solution)/shard_map/all_to_all | solution.py:185
  115.3 0.1 relay.1
  115.4 17.8 %all-gather.1.s_ref = f32[8,1,128]{2,1,0:T(1,128)S(1)} all-gather(f32[1,1,128]{2,1,0:T(1,128)S(1)} %bitcast.3), channel_id=2, replica_groups={{1,33,65,97,129,161,193,225},{9,41,73,105,137,169,201,233},{17,49,81,11..., dimensions={0}, use_global_device_ids=true | all-gather | bytes 4608 | tf_op jit(solution)/shard_map/all_gather | solution.py:194
  133.2 1.3 collective-permute-start
  134.5 0.8 collective-permute-done.t_ref
  135.3 0.0 copy-done.1
  135.3 0.7 update.1
Async XLA Ops:
  46.5 50.9 %copy-start = (bf16[512,1024]{1,0:T(8,128)(2,1)S(1)}, bf16[512,1024]{1,0:T(8,128)(2,1)}, u32[]{:S(2)}) copy-start(bf16[512,1024]{1,0:T(8,128)(2,1)} %r_ref.1) | copy-start | bytes 3145732
  46.5 88.8 %copy-start.1 = (f32[4,1024]{1,0:T(4,128)S(1)}, f32[4,1024]{1,0:T(4,128)}, u32[]{:S(2)}) copy-start(f32[4,1024]{1,0:T(4,128)} %m_ref.1) | copy-start | bytes 49156
  133.2 2.1 %collective-permute-start = (f32[8,1,128]{2,1,0:T(1,128)S(1)}, f32[8,1,128]{2,1,0:T(1,128)S(1)}, u32[]{:S(2)}, u32[]{:S(2)}) collective-permute-start(f32[8,1,128]{2,1,0:T(1,128)S(1)} %all-gather.1.s_ref), channel_id=1, source_target_pairs={{1,0},{3,2},{5,4},{7,6},{9,8},{11,10},{13,12},{15,14},{17,16},{19,... | collective-permute-start | bytes 12296 | tf_op jit(solution)/shard_map/ppermute | solution.py:195
